TPU v7x, 256 devices: a 4x2x16 block of a 4x16x16 slice. The times are simulated.
256 devices in a mesh: ens: 2 (over y), gx: 128 (over x, z, core).
Axes of the slice: x: 4, y: 2, z: 16, core: 2. Of those that a mesh axis runs over, the one named last changes fastest.
The devices are a block of a 4x16x16 slice.
Arguments:
- model_state: float32 [8, 4, 2560, 2560], P('ens', None, 'gx'), parts along dimension 0, may hold values from -6 to 6
- driving: float32 [8, 4, 2560, 2560], P('ens', None, 'gx'), parts along dimension 0, may hold values from -12 to 12
- mode_east: int32 [30], replicated, may hold values from 1 to 60, as said below
- mode_north: int32 [30], replicated, may hold values from 1 to 60, as said below
- level_class: int32 [4], replicated, may hold values from 0 to 7
- nudge_table: float32 [8, 4], replicated, may hold values from 0.05 to 0.5
Outputs:
- nudged: float32 [8, 4, 2560, 2560], P('ens', None, 'gx'), parts along dimension 0
- residual_log: float32 [8, 4], P('ens'), parts along dimension 0
There are 2 independent parts, one for each index of `ens`. A program takes and returns all parts, laid end to end along the dimension named above; an argument that names none is the same for every part. Nothing has to cross between parts.
Inputs may be any that keep to these rules, and one draw needn't show every extreme that they name: `mode_east`: 30 distinct wavenumbers in increasing order, the first 1 and the last 60. `mode_north`: 30 distinct wavenumbers in increasing order, the first 1 and the last 60.
All inputs are finite; a program needn't handle non-finite values.
Results may differ from a plain program's by a relative error of at most 0.0001.
Values sent between devices are 32-bit elements; how exact they have to be, the bound alone decides.
A program may use at most 128 MiB of HBM per device.

v0:
```python
import jax
import jax.numpy as jnp
from jax import lax
from jax.sharding import Mesh
from jax.sharding import PartitionSpec as P

ITERS = 4
GX = ("gx_0", "gx_1", "gx_2")


DIFFUSION = 0.24


def by_axis(value, axes):
    for axis in axes:
        value = lax.psum(value, axis)
    return value


def extended_2(cells, sides, width):
    for axis, dim in sides:
        count = lax.axis_size(axis)
        ends = count - 1
        head = lax.slice_in_dim(cells, 0, width, axis=dim)
        tail = lax.slice_in_dim(cells, cells.shape[dim] - width, cells.shape[dim], axis=dim)
        cells = jnp.concatenate(
            [
                lax.ppermute(tail, axis, [(i, (i + 1) % count) for i in range(ends)]),
                cells,
                lax.ppermute(head, axis, [((i + 1) % count, i) for i in range(ends)]),
            ],
            axis=dim,
        )
    return cells


def sine_table(wavenums, first_cell, span_cols, grid_cells):
    places = first_cell + lax.iota(jnp.int32, span_cols) + 1
    phases = wavenums[:, None] * places[None, :] % (2 * (grid_cells + 1))
    return jnp.sin(phases.astype(jnp.float32) * (jnp.pi / (grid_cells + 1)))


def laplace(extended):
    centre = extended[:, :, 1:-1]
    padded = jnp.pad(centre, ((0, 0), (0, 0), (0, 0), (1, 1)))
    return (
        extended[:, :, 2:]
        + extended[:, :, :-2]
        + padded[:, :, :, 2:]
        + padded[:, :, :, :-2]
        - 4.0 * centre
    )


def local(model_state, driving, mode_east, mode_north, level_class, nudge_table):
    fields, levels, columns, north_cells = model_state.shape
    tiles = lax.axis_size(GX)
    first_col = lax.axis_index(GX) * columns
    total_east = columns * tiles
    scale_norm = 4.0 / ((total_east + 1) * (north_cells + 1))
    cell_count = float(levels * total_east * north_cells)
    table_north = sine_table(mode_north, 0, north_cells, north_cells)
    table_own = sine_table(mode_east, first_col, columns, total_east)
    one_hot = (level_class[:, None] == lax.iota(jnp.int32, nudge_table.shape[0])[None, :]).astype(
        jnp.float32
    )
    weights = jnp.dot(one_hot, nudge_table, precision=lax.Precision.HIGHEST).T[:, :, None, None]
    records = []
    extended = extended_2(model_state, ((GX, 2),), ITERS)
    for substep in range(ITERS):
        reach_now = ITERS - substep
        current = extended[:, :, reach_now : reach_now + columns]
        along_north = jnp.dot(
            (driving - current).reshape(-1, north_cells),
            table_north.T,
            precision=lax.Precision.HIGHEST,
        )
        along_north = along_north.reshape(fields, levels, columns, -1)
        mode_partial_value = (
            jnp.einsum("flxb,ax->flab", along_north, table_own, precision=lax.Precision.HIGHEST)
            * scale_norm
        )
        coeffs = by_axis(mode_partial_value, GX)
        lead_col = first_col - (reach_now - 1)
        span_cols = columns + 2 * (reach_now - 1)
        table_wide = sine_table(mode_east, lead_col, span_cols, total_east)
        global_col = lead_col + lax.iota(jnp.int32, span_cols)
        inside = ((global_col >= 0) & (global_col < total_east))[None, None, :, None]
        partial_value = jnp.einsum(
            "flab,ax->flxb", coeffs, table_wide, precision=lax.Precision.HIGHEST
        )
        rebuild_span_cols = table_wide.shape[1]
        flat = jnp.dot(
            partial_value.reshape(-1, partial_value.shape[-1]),
            table_north,
            precision=lax.Precision.HIGHEST,
        )
        updated = (
            extended[:, :, 1:-1]
            + flat.reshape(fields, levels, rebuild_span_cols, north_cells) * weights
            + DIFFUSION * laplace(extended)
        )
        extended = jnp.where(inside, updated, 0.0)
        current = extended[:, :, reach_now - 1 : reach_now - 1 + columns]
        remain = driving - current
        squares = jnp.sum(remain * remain, axis=(1, 2, 3))
        records.append(by_axis(squares, GX))
    stacked = jnp.stack(records)
    return (current, jnp.sqrt(stacked / cell_count))


def solution(mesh):
    finer = Mesh(mesh.devices.reshape(mesh.shape["ens"], 4, 16, 2), ("ens", "gx_0", "gx_1", "gx_2"))
    in_specs = (P("ens", None, GX, None), P("ens", None, GX, None), P(), P(), P(), P())
    out_specs = (P("ens", None, GX, None), P("ens", None))
    return jax.shard_map(local, mesh=finer, in_specs=in_specs, out_specs=out_specs, check_vma=False)
```

profile of v0, /device:TPU:33, one launch (start us, length us, event | category | flops | bytes accessed | tf_op | source)
XLA Modules:
  0.0 493.7 jit_solution(17798823323414789324)
XLA Ops:
  6.9 5.7 %collective-permute-start = (f32[4,4,4,2560]{3,2,1,0:T(4,128)}, f32[4,4,4,2560]{3,2,1,0:T(4,128)}, u32[]{:S(2)}, u32[]{:S(2)}) collective-permute-start(f32[4,4,4,2560]{3,2,1,0:T(4,128)} %get-tuple-element.20), channel_id=1, source_target_pairs={{0,1},{1,2},{2,3},{3,4},{4,5},{5,6},{6,7},{7,8},{8,9},{9,10},{10,1... | collective-permute-start | bytes 1966088 | tf_op jit(solution)/shard_map/ppermute | solution.py:28
  12.7 18.8 %collective-permute-start.1 = (f32[4,4,4,2560]{3,2,1,0:T(4,128)}, f32[4,4,4,2560]{3,2,1,0:T(4,128)}, u32[]{:S(2)}, u32[]{:S(2)}) collective-permute-start(f32[4,4,4,2560]{3,2,1,0:T(4,128)} %get-tuple-element.21), channel_id=1, source_target_pairs={{1,0},{2,1},{3,2},{4,3},{5,4},{6,5},{7,6},{8,7},{9,8},{10,9},{11,1... | collective-permute-start | bytes 1966088 | tf_op jit(solution)/shard_map/ppermute | solution.py:30
  43.3 14.7 %psum.168 = f32[4,4,30,30]{3,1,0,2:T(4,128)S(1)} all-reduce(f32[4,4,30,30]{3,1,0,2:T(4,128)} %bitcast.73), channel_id=1, replica_groups=mesh['ens'=2,'gx_0'=4,'gx_1'=16,'gx_2'=2] {'gx_0'}, use_global_device_ids=true, to_apply=%region_0.1 | all-reduce | flops 14400 | bytes 115200 | tf_op jit(solution)/shard_map/psum | solution.py:16
  58.9 47.4 %psum.169 = f32[4,4,30,30]{3,1,0,2:T(4,128)} all-reduce(f32[4,4,30,30]{3,1,0,2:T(4,128)S(1)} %psum.168), channel_id=1, replica_groups=mesh['ens'=2,'gx_0'=4,'gx_1'=16,'gx_2'=2] {'gx_1'}, use_global_device_ids=true, to_apply=%region_1.2 | all-reduce | flops 14400 | bytes 115200 | tf_op jit(solution)/shard_map/psum | solution.py:16
  107.1 23.6 %psum.170 = f32[4,4,30,30]{3,1,0,2:T(4,128)S(1)} all-reduce(f32[4,4,30,30]{3,1,0,2:T(4,128)} %psum.169), channel_id=1, replica_groups=mesh['ens'=2,'gx_0'=4,'gx_1'=16,'gx_2'=2] {'gx_2'}, use_global_device_ids=true, to_apply=%region_2.3 | all-reduce | flops 14400 | bytes 115200 | tf_op jit(solution)/shard_map/psum | solution.py:16
  136.0 6.8 %fusion.5 = f32[4,4,26,2560]{3,2,1,0:T(8,128)S(1)} fusion(f32[4,4,26,2560]{3,2,1,0:T(8,128)S(1)} %slice.106, f32[4,4,28,2560]{3,2,1,0:T(8,128)S(1)} %pad_maximum_fusion, f32[4,4,26,30]{3,2,1,0:T(8,128)S(1)} %convolution_bitcast_fusion, f32[4,4]{1,0:T(4,128)S(1)} %copy.11, pred[26]{0:T(512)(128)(4,1)S(1)} %compare_and_fusion, s32[2560]{0:T(1024)S(1)} %iota_add_fusion, ...), kind=kOutput, calls=%fused_computation.7 | convolution fusion | flops 394726400 | bytes 17099730 | tf_op jit(solution)/shard_map/dot_general | solution.py:93
  142.8 5.7 %fusion.32 = f32[4,4,20,30]{3,2,1,0:T(8,128)S(1)} fusion(f32[4,4,20,2560]{3,1,2,0:T(4,128)S(1)} %copy-done.1, f32[4,4,26,2560]{3,2,1,0:T(8,128)S(1)} %fusion.5, s32[2560]{0:T(1024)S(1)} %iota_add_fusion, s32[30]{0:T(128)S(1)} %copy-done.7), kind=kOutput, calls=%fused_computation.55 | convolution fusion | flops 296422400 | bytes 7260160 | tf_op jit(solution)/shard_map/dot_general | solution.py:73
  151.7 14.8 %psum.171 = f32[4,4,30,30]{3,1,0,2:T(4,128)} all-reduce(f32[4,4,30,30]{3,1,0,2:T(4,128)S(1)} %bitcast.74), channel_id=1, replica_groups=mesh['ens'=2,'gx_0'=4,'gx_1'=16,'gx_2'=2] {'gx_0'}, use_global_device_ids=true, to_apply=%region_3.4 | all-reduce | flops 14400 | bytes 115200 | tf_op jit(solution)/shard_map/psum | solution.py:16
  166.5 42.7 %psum.172 = f32[4,4,30,30]{3,1,0,2:T(4,128)} all-reduce(f32[4,4,30,30]{3,1,0,2:T(4,128)} %psum.171), channel_id=1, replica_groups=mesh['ens'=2,'gx_0'=4,'gx_1'=16,'gx_2'=2] {'gx_1'}, use_global_device_ids=true, to_apply=%region_4.5 | all-reduce | flops 14400 | bytes 115200 | tf_op jit(solution)/shard_map/psum | solution.py:16
  209.2 21.6 %psum.173 = f32[4,4,30,30]{3,1,0,2:T(4,128)S(1)} all-reduce(f32[4,4,30,30]{3,1,0,2:T(4,128)} %psum.172), channel_id=1, replica_groups=mesh['ens'=2,'gx_0'=4,'gx_1'=16,'gx_2'=2] {'gx_2'}, use_global_device_ids=true, to_apply=%region_5.6 | all-reduce | flops 14400 | bytes 115200 | tf_op jit(solution)/shard_map/psum | solution.py:16
  232.0 10.2 %fusion.12 = f32[4,4,24,2560]{3,2,1,0:T(8,128)S(1)} fusion(f32[4,4,24,2560]{3,2,1,0:T(8,128)} %slice.109, f32[4,4,24,30]{3,2,1,0:T(8,128)S(1)} %convolution_bitcast_fusion.3, f32[4,4,26,2560]{3,2,1,0:T(8,128)} %copy-done.5, f32[4,4]{1,0:T(4,128)S(1)} %copy.11, pred[24]{0:T(512)(128)(4,1)} %compare_and_fusion.1, s32[2560]{0:T(1024)S(1)} %iota_add_fusion, ...), kind=kOutput, calls=%fused_computation.19 | convolution fusion | flops 364416000 | bytes 15785168 | tf_op jit(solution)/shard_map/dot_general | solution.py:93
  242.2 5.2 %fusion.33 = f32[4,4,20,30]{3,2,1,0:T(8,128)S(1)} fusion(f32[4,4,20,2560]{3,1,2,0:T(4,128)S(1)} %copy-done.1, f32[4,4,24,2560]{3,2,1,0:T(8,128)S(1)} %fusion.12, s32[2560]{0:T(1024)S(1)} %iota_add_fusion, s32[30]{0:T(128)S(1)} %copy-done.7), kind=kOutput, calls=%fused_computation.56 | convolution fusion | flops 296422400 | bytes 7257720 | tf_op jit(solution)/shard_map/dot_general | solution.py:73
  250.5 16.3 %psum.174 = f32[4,4,30,30]{3,1,0,2:T(4,128)} all-reduce(f32[4,4,30,30]{3,1,0,2:T(4,128)S(1)} %bitcast.75), channel_id=1, replica_groups=mesh['ens'=2,'gx_0'=4,'gx_1'=16,'gx_2'=2] {'gx_0'}, use_global_device_ids=true, to_apply=%region_6.7 | all-reduce | flops 14400 | bytes 115200 | tf_op jit(solution)/shard_map/psum | solution.py:16
  266.8 43.6 %psum.175 = f32[4,4,30,30]{3,1,0,2:T(4,128)} all-reduce(f32[4,4,30,30]{3,1,0,2:T(4,128)} %psum.174), channel_id=1, replica_groups=mesh['ens'=2,'gx_0'=4,'gx_1'=16,'gx_2'=2] {'gx_1'}, use_global_device_ids=true, to_apply=%region_7.8 | all-reduce | flops 14400 | bytes 115200 | tf_op jit(solution)/shard_map/psum | solution.py:16
  310.5 22.8 %psum.176 = f32[4,4,30,30]{3,1,0,2:T(4,128)S(1)} all-reduce(f32[4,4,30,30]{3,1,0,2:T(4,128)} %psum.175), channel_id=1, replica_groups=mesh['ens'=2,'gx_0'=4,'gx_1'=16,'gx_2'=2] {'gx_2'}, use_global_device_ids=true, to_apply=%region_8.9 | all-reduce | flops 14400 | bytes 115200 | tf_op jit(solution)/shard_map/psum | solution.py:16
  334.4 9.9 %fusion.13 = f32[4,4,22,2560]{3,2,1,0:T(8,128)S(1)} fusion(f32[4,4,22,2560]{3,2,1,0:T(8,128)} %slice.113, f32[4,4,22,30]{3,2,1,0:T(8,128)S(1)} %convolution_bitcast_fusion.2, f32[4,4,24,2560]{3,2,1,0:T(8,128)} %copy-done.3, f32[4,4]{1,0:T(4,128)S(1)} %copy.11, pred[22]{0:T(512)(128)(4,1)} %compare_and_fusion.2, s32[2560]{0:T(1024)S(1)} %iota_add_fusion, ...), kind=kOutput, calls=%fused_computation.20 | convolution fusion | flops 334105600 | bytes 14470606 | tf_op jit(solution)/shard_map/dot_general | solution.py:93
  344.4 5.2 %fusion.31 = f32[4,4,20,30]{3,2,1,0:T(8,128)S(1)} fusion(f32[4,4,20,2560]{3,1,2,0:T(4,128)S(1)} %copy-done.1, s32[2560]{0:T(1024)S(1)} %iota_add_fusion, s32[30]{0:T(128)S(1)} %copy-done.7, f32[4,4,22,2560]{3,2,1,0:T(8,128)S(1)} %fusion.13), kind=kOutput, calls=%fused_computation.54 | convolution fusion | flops 296422400 | bytes 6930040 | tf_op jit(solution)/shard_map/dot_general | solution.py:73
  352.7 14.7 %psum.177 = f32[4,4,30,30]{3,1,0,2:T(4,128)} all-reduce(f32[4,4,30,30]{3,1,0,2:T(4,128)S(1)} %bitcast.76), channel_id=1, replica_groups=mesh['ens'=2,'gx_0'=4,'gx_1'=16,'gx_2'=2] {'gx_0'}, use_global_device_ids=true, to_apply=%region_9.10 | all-reduce | flops 14400 | bytes 115200 | tf_op jit(solution)/shard_map/psum | solution.py:16
  367.4 42.9 %psum.178 = f32[4,4,30,30]{3,1,0,2:T(4,128)} all-reduce(f32[4,4,30,30]{3,1,0,2:T(4,128)} %psum.177), channel_id=1, replica_groups=mesh['ens'=2,'gx_0'=4,'gx_1'=16,'gx_2'=2] {'gx_1'}, use_global_device_ids=true, to_apply=%region_10.11 | all-reduce | flops 14400 | bytes 115200 | tf_op jit(solution)/shard_map/psum | solution.py:16
  410.2 22.0 %psum.179 = f32[4,4,30,30]{3,1,0,2:T(4,128)S(1)} all-reduce(f32[4,4,30,30]{3,1,0,2:T(4,128)} %psum.178), channel_id=1, replica_groups=mesh['ens'=2,'gx_0'=4,'gx_1'=16,'gx_2'=2] {'gx_2'}, use_global_device_ids=true, to_apply=%region_11.12 | all-reduce | flops 14400 | bytes 115200 | tf_op jit(solution)/shard_map/psum | solution.py:16
  432.7 15.7 %multiply_reduce_fusion.2 = (f32[4]{0:T(128)S(1)}, f32[4]{0:T(128)S(1)}, f32[4]{0:T(128)S(1)}, f32[4]{0:T(128)S(1)}, f32[4,4,20,2560]{3,2,1,0:T(8,128)S(1)}) fusion(f32[4,4,26,2560]{3,2,1,0:T(8,128)} %copy-done.5, f32[4,4,20,2560]{3,1,2,0:T(4,128)S(1)} %copy-done.1, f32[4,4,24,2560]{3,2,1,0:T(8,128)} %copy-done.3, f32[4,4,22,2560]{3,2,1,0:T(8,128)} %copy-done.4, ...), kind=kOutput, calls=%fused_computation.53 | convolution fusion | flops 313625600 | bytes 26263308 | tf_op jit(solution)/shard_map/dot_general | solution.py:93
  452.2 7.7 %all-reduce.5 = (f32[4]{0:T(128)S(1)}, f32[4]{0:T(128)S(1)}, f32[4]{0:T(128)S(1)}, f32[4]{0:T(128)S(1)}) all-reduce(f32[4]{0:T(128)S(1)} %get-tuple-element.7, f32[4]{0:T(128)S(1)} %get-tuple-element.6, f32[4]{0:T(128)S(1)} %get-tuple-element.5, f32[4]{0:T(128)S(1)} %get-tuple-element.4), channel_id=1, replica_groups=mesh['ens'=2,'gx_0'=4,'gx_1'=16,'gx_2'=2] {'gx_0'}, use_global_device_ids=true, to_apply=%region_25.26 | all-reduce | flops 16 | bytes 128 | tf_op jit(solution)/shard_map/psum | solution.py:16
  459.9 21.4 %all-reduce.4 = (f32[4]{0:T(128)S(1)}, f32[4]{0:T(128)S(1)}, f32[4]{0:T(128)S(1)}, f32[4]{0:T(128)S(1)}) all-reduce(f32[4]{0:T(128)S(1)} %get-tuple-element.12, f32[4]{0:T(128)S(1)} %get-tuple-element.13, f32[4]{0:T(128)S(1)} %get-tuple-element.14, ...), channel_id=1, replica_groups=mesh['ens'=2,'gx_0'=4,'gx_1'=16,'gx_2'=2] {'gx_1'}, use_global_device_ids=true, to_apply=%region_26.27 | all-reduce | flops 16 | bytes 128 | tf_op jit(solution)/shard_map/psum | solution.py:16
  481.3 11.6 %all-reduce.6 = (f32[1,4]{1,0:T(1,128)S(1)}, f32[1,4]{1,0:T(1,128)S(1)}, f32[1,4]{1,0:T(1,128)S(1)}, f32[1,4]{1,0:T(1,128)S(1)}) all-reduce(f32[1,4]{1,0:T(1,128)S(1)} %bitcast.77, f32[1,4]{1,0:T(1,128)S(1)} %bitcast.78, f32[1,4]{1,0:T(1,128)S(1)} %bitcast.79, ...), channel_id=1, replica_groups=mesh['ens'=2,'gx_0'=4,'gx_1'=16,'gx_2'=2] {'gx_2'}, use_global_device_ids=true, to_apply=%region_27.28 | all-reduce | flops 16 | bytes 128 | tf_op jit(solution)/shard_map/psum | solution.py:16
  (54 shorter events, 41.4 us)
Async XLA Ops:
  0.6 57.4 %copy-start = (f32[8,4]{0,1:T(4,128)S(1)}, f32[8,4]{0,1:T(4,128)}, u32[]{:S(2)}) copy-start(f32[8,4]{0,1:T(4,128)} %param.11) | copy-start | bytes 388
  0.6 32.9 %copy-start.1 = (f32[4,4,20,2560]{3,1,2,0:T(4,128)S(1)}, f32[4,4,20,2560]{3,1,2,0:T(4,128)}, u32[]{:S(2)}) copy-start(f32[4,4,20,2560]{3,1,2,0:T(4,128)} %param.7) | copy-start | bytes 9830404
  3.8 1.9 copy-start.2
  6.9 124.9 %collective-permute-start = (f32[4,4,4,2560]{3,2,1,0:T(4,128)}, f32[4,4,4,2560]{3,2,1,0:T(4,128)}, u32[]{:S(2)}, u32[]{:S(2)}) collective-permute-start(f32[4,4,4,2560]{3,2,1,0:T(4,128)} %get-tuple-element.20), channel_id=1, source_target_pairs={{0,1},{1,2},{2,3},{3,4},{4,5},{5,6},{6,7},{7,8},{8,9},{9,10},{10,1... | collective-permute-start | bytes 1966088 | tf_op jit(solution)/shard_map/ppermute | solution.py:28
  12.7 119.2 %collective-permute-start.1 = (f32[4,4,4,2560]{3,2,1,0:T(4,128)}, f32[4,4,4,2560]{3,2,1,0:T(4,128)}, u32[]{:S(2)}, u32[]{:S(2)}) collective-permute-start(f32[4,4,4,2560]{3,2,1,0:T(4,128)} %get-tuple-element.21), channel_id=1, source_target_pairs={{1,0},{2,1},{3,2},{4,3},{5,4},{6,5},{7,6},{8,7},{9,8},{10,9},{11,1... | collective-permute-start | bytes 1966088 | tf_op jit(solution)/shard_map/ppermute | solution.py:30
  33.6 3.6 copy-start.7
  37.2 4.8 copy-start.6
  37.2 20.9 %copy-start.8 = (s32[4]{0:T(128)S(1)}, s32[4]{0:T(128)}, u32[]{:S(2)}) copy-start(s32[4]{0:T(128)} %param.10) | copy-start | bytes 52
  142.8 5.7 %copy-start.5 = (f32[4,4,26,2560]{3,2,1,0:T(8,128)}, f32[4,4,26,2560]{3,2,1,0:T(8,128)S(1)}, u32[]{:S(2)}) copy-start(f32[4,4,26,2560]{3,2,1,0:T(8,128)S(1)} %fusion.5) | copy-start | bytes 12779524
  242.2 5.2 %copy-start.3 = (f32[4,4,24,2560]{3,2,1,0:T(8,128)}, f32[4,4,24,2560]{3,2,1,0:T(8,128)S(1)}, u32[]{:S(2)}) copy-start(f32[4,4,24,2560]{3,2,1,0:T(8,128)S(1)} %fusion.12) | copy-start | bytes 11796484
  344.3 5.2 %copy-start.4 = (f32[4,4,22,2560]{3,2,1,0:T(8,128)}, f32[4,4,22,2560]{3,2,1,0:T(8,128)S(1)}, u32[]{:S(2)}) copy-start(f32[4,4,22,2560]{3,2,1,0:T(8,128)S(1)} %fusion.13) | copy-start | bytes 10813444
where the time goes:
time: 502 us; the launch traced here: 494 us
  blocking collectives  368 us (73%)
  matrix products  69.6 us (14%)
  starting transfers between devices  24.5 us (5%)
  local copies, waits for them, and re-layouts  20.5 us (4%)
  other arithmetic  10.1 us (2%)
    psum x15, blocking collectives, by_axis(): value = lax.psum(value, axis)  368 us
    dot_general x4, matrix products, local(): jnp.dot(partial_value.reshape(-1, partial_value.shape[-1]), table_north,...  42.6 us
    dot_general x4, matrix products, local(): jnp.dot((driving - current).reshape(-1, north_cells), table_north.T, prec...  20.9 us
    ppermute x1, starting transfers between devices, extended_2(): lax.ppermute(head, axis, [((i + 1) % count, i) for i in range(ends)])  18.8 us
    unnamed x24, local copies, waits for them, and re-layouts  10.2 us
  transfers between devices with their start and end apart: 2, of which 0 were waited for; matrix products, arithmetic and copies ran while one was open for 3% of the time, Pallas kernels for 0%

commit v1 on v0

v1 whole, which is shorter than its diff:
```python
import functools

import jax
import jax.numpy as jnp
import numpy as np
from jax import lax
from jax.experimental import pallas as pl
from jax.experimental.pallas import tpu as pltpu
from jax.sharding import PartitionSpec as P

ITERS = 4
DIFFUSION = 0.24
CORES = 2
RING = 16
MESH = pl.DeviceIdType.MESH
HIGHEST = lax.Precision.HIGHEST
F32 = jnp.float32
LANES = 128
HALO = 4
PAD = 8


def iota(shape, dim):
    return lax.broadcasted_iota(jnp.int32, shape, dim)


def pick(ref, which, count):
    out = jnp.zeros(which.shape, F32)
    for i in range(count):
        out = jnp.where(which == i, ref[i].astype(F32), out)
    return out


def sine(product, period):
    turns = jnp.floor(product * (1.0 / period) + 0.5)
    x = (product - turns * period) * (np.pi / period)
    odd = turns - 2.0 * jnp.floor(turns * 0.5)
    y = x * x
    poly = 1.0 / 6227020800.0
    for c in (-1.0 / 39916800.0, 1.0 / 362880.0, -1.0 / 5040.0, 1.0 / 120.0, -1.0 / 6.0, 1.0):
        poly = poly * y + c
    return x * poly * (1.0 - 2.0 * odd)


def split(value):
    high = value.astype(jnp.bfloat16)
    return high, (value - high.astype(F32)).astype(jnp.bfloat16)


def kernel(
    tiles, u_hbm, d_hbm, me_ref, mn_ref, lc_ref, nt_ref, o_hbm, res_ref,
    U, D, O, W, T, CA, RA, QB, DB, QC, SB, EB, ACC, PS,
    in_sem, out_sem, hs_sem, hr_sem, as_sem, ar_sem, qs_sem, qr_sem, ds_sem, dr_sem,
    cs_sem, cr_sem, ss_sem, sr_sem, es_sem, er_sem,
):
    fields, cols, levels, north = u_hbm.shape
    kx, ky = me_ref.shape[0], mn_ref.shape[0]
    east = cols * tiles
    members = tiles // RING
    chunks = north // LANES
    blocks = chunks // 2
    wide = cols + 2 * HALO
    rows = 8 * blocks
    high_rows = rows + 2 * PAD
    own = pl.ds(HALO, cols)
    g = lax.axis_index("gx")
    core = lax.rem(g, CORES)
    z = lax.rem(g // CORES, RING)
    xi = g // (CORES * RING)
    me = xi * CORES + core

    def member(i):
        return {"gx": ((i // CORES) * RING + z) * CORES + lax.rem(i, CORES)}

    def ring(i):
        return {"gx": (xi * RING + i) * CORES + core}

    right = {"gx": lax.rem(g + 1, tiles)}
    left = {"gx": lax.rem(g + tiles - 1, tiles)}
    others = [lax.rem(me + k, members) for k in range(1, members)]
    far_first = sorted(range(1, RING), key=lambda k: -min(k, RING - k))
    spots = [lax.rem(z + k, RING) for k in far_first]

    u_view = U.reshape(fields, wide, high_rows // levels, levels, LANES)
    d_view = D.reshape(fields, cols, chunks, levels, LANES)
    o_view = O.reshape(fields, cols, chunks, levels, LANES)
    skip = PAD // levels
    for h in range(0, fields, 2):
        for i in range(2):
            for f in (h, h + 1):
                for t in range(chunks):
                    hbm, dst = (
                        (u_hbm, u_view.at[f, own, skip + t]) if i == 0 else (d_hbm, d_view.at[f, :, t])
                    )
                    pltpu.make_async_copy(
                        hbm.at[f, :, :, pl.ds(t * LANES, LANES)], dst, in_sem.at[i, f]
                    ).start()

    def loaded(i, f):
        ref = U.at[f, own, pl.ds(PAD, rows)] if i == 0 else D.at[f]
        pltpu.make_async_copy(ref, ref, in_sem.at[i, f]).wait()

    barrier = pltpu.get_barrier_semaphore()
    greeted = [member(i) for i in others] + [ring(i) for i in spots] + [left, right]
    for who in greeted:
        pl.semaphore_signal(barrier, inc=1, device_id=who, device_id_type=MESH)

    row32 = iota((32, LANES), 0)
    lane32 = iota((32, LANES), 1)
    modes_n = pick(mn_ref, row32, ky)
    for c in range(chunks):
        place = (lane32 + (c * LANES + 1)).astype(F32)
        high, low = split(sine(modes_n * place, float(north + 1)))
        at = pl.ds(c * LANES, LANES)
        both = jnp.concatenate([high, low], axis=0)
        T[0:64, at] = both
        T[64:128, at] = both
    first = g * cols
    count = 8 * cols
    grid_rows = 8 * ((count + LANES - 1) // LANES) * (LANES // 8)
    row_m, lane_m = iota((LANES, grid_rows), 0), iota((LANES, grid_rows), 1)
    mode_m = pick(me_ref, iota((LANES, LANES), 0) % 32, kx)
    mode_m = jnp.concatenate([mode_m] * (grid_rows // LANES), axis=1)
    to_modes = jnp.where(
        (lane_m < count) & (row_m // 32 == lane_m % 4),
        sine(mode_m * (lane_m // 8 + first + 1).astype(F32), float(east + 1)), 0.0,
    )
    row_g, lane_g = iota((count, LANES), 0), iota((count, LANES), 1)
    mode_g = jnp.concatenate([pick(me_ref, iota((8, LANES), 1) % 32, kx)] * cols, axis=0)
    to_grid = jnp.where(
        row_g % 4 == lane_g // 32,
        sine(mode_g * (row_g // 8 + first + 1).astype(F32), float(east + 1)), 0.0,
    )
    edge = jnp.zeros((wide, PAD, LANES), F32)
    for f in range(fields):
        U[f, :, 0:PAD] = edge
        U[f, :, PAD + rows : high_rows] = edge
    for s in range(2):
        W[s, :, 0:PAD] = edge
        W[s, :, PAD + rows : high_rows] = edge

    row16 = iota((16, LANES), 0)
    lane16 = iota((16, LANES), 1)
    a16 = row16 + jnp.where(lane16 >= 64, 16, 0)
    b16 = lane16 % 32
    upper = lane16 % 64 >= 32
    half_e = sine(pick(me_ref, a16, kx), 2.0 * (east + 1))
    half_n = sine(pick(mn_ref, b16, ky), 2.0 * (north + 1))
    fade = (4.0 * DIFFUSION) * (half_e * half_e + half_n * half_n)
    lam = 1.0 - fade
    f_low = 2 * (me // levels)
    my_class = lc_ref[lax.rem(me, levels)]
    w16 = jnp.where(upper, nt_ref[my_class, f_low + 1], nt_ref[my_class, f_low])

    def substeps(r, d):
        t = jnp.zeros_like(r)
        v = r
        out = []
        for _ in range(ITERS):
            t = lam * t + w16 * r
            r = (lam - w16) * r + fade * d
            v = lam * v + fade * d
            out.append((t, r, v))
        return out

    norm = 4.0 / ((east + 1) * (north + 1))
    odd_chunk = row_g % 8 >= 4
    contract_lanes = (((1,), (1,)), ((), ()))
    for h in range(0, fields, 2):
        for f in (h, h + 1):
            loaded(0, f)
        for f in (h, h + 1):
            loaded(1, f)
        acc_r = acc_d = None
        held = []
        for k in range(blocks):
            at = pl.ds(8 * k, 8)
            d = D[h : h + 2, :, at]
            r = d - U[h : h + 2, own, pl.ds(PAD + 8 * k, 8)]
            high, low = split(r.reshape(2 * count, LANES))
            table = jnp.concatenate(
                [T[0:64, pl.ds((2 * k + p) * LANES, LANES)] for p in range(2)], axis=0
            )
            out = lax.dot_general(
                jnp.concatenate([high, low], axis=1), jnp.concatenate([table, table], axis=1),
                contract_lanes, preferred_element_type=F32,
            )
            acc_r = out if acc_r is None else acc_r + out
            held.append((d.reshape(2 * count, LANES).astype(jnp.bfloat16), table))
            if len(held) == 2:
                out = lax.dot_general(
                    jnp.concatenate([held[0][0], held[1][0]], axis=1),
                    jnp.concatenate([held[0][1], held[1][1]], axis=1),
                    contract_lanes, preferred_element_type=F32,
                )
                acc_d = out if acc_d is None else acc_d + out
                held = []
        mix = jnp.zeros((count, LANES), F32)
        for i, acc in enumerate((acc_r, acc_d)):
            acc = acc + pltpu.roll(acc, 32, 1)
            for j in range(2):
                mine = acc[j * count : (j + 1) * count]
                slot = 2 * i + j
                even, odd = ((slot - 1) % 4) * 32, ((slot + 1) % 4) * 32
                even = pltpu.roll(mine, even, 1) if even else mine
                odd = pltpu.roll(mine, odd, 1) if odd else mine
                mix = jnp.where(lane_g // 32 == slot, jnp.where(odd_chunk, odd, even), mix)
        if grid_rows > count:
            mix = jnp.concatenate([mix, jnp.zeros((grid_rows - count, LANES), F32)], axis=0)
        modal = norm * jnp.dot(to_modes, mix, precision=HIGHEST, preferred_element_type=F32)
        for l in range(levels):
            CA[(h // 2) * levels + l] = modal[32 * l : 32 * l + 32]

    pl.semaphore_wait(barrier, len(greeted))

    def send(src, dst, send_sem, recv_sem, who):
        copy = pltpu.make_async_remote_copy(
            src_ref=src, dst_ref=dst, send_sem=send_sem, recv_sem=recv_sem,
            device_id=who, device_id_type=MESH,
        )
        copy.start()
        return copy

    def landed(ref, sem, who):
        pltpu.make_async_remote_copy(
            src_ref=ref, dst_ref=ref, send_sem=sem, recv_sem=sem,
            device_id=who, device_id_type=MESH,
        ).wait_recv()

    sent = []
    for i in others:
        sent.append(send(CA.at[i], RA.at[me], as_sem.at[i], ar_sem.at[me], member(i)))
    body_rows = pl.ds(PAD, rows)
    for f in range(fields):
        sent.append(send(
            U.at[f, pl.ds(cols, HALO), body_rows], U.at[f, pl.ds(0, HALO), body_rows],
            hs_sem.at[0, f], hr_sem.at[0, f], right,
        ))
        sent.append(send(
            U.at[f, pl.ds(HALO, HALO), body_rows], U.at[f, pl.ds(HALO + cols, HALO), body_rows],
            hs_sem.at[1, f], hr_sem.at[1, f], left,
        ))
    RA[me] = CA[me]
    for i in others:
        landed(RA.at[i], ar_sem.at[i], member(i))
    total = RA[0]
    for i in range(1, members):
        total = total + RA[i]
    turned = pltpu.roll(total, 64, 1)
    left_half = lane16 < 64
    r_part = jnp.where(left_half, total[0:16], turned[16:32])
    d_part = jnp.where(left_half, turned[0:16], total[16:32])
    QB[z] = substeps(r_part, d_part)[-1][0]
    DB[z] = d_part
    for i in spots:
        sent.append(send(QB.at[z], QB.at[z], qs_sem.at[i], qr_sem.at[z], ring(i)))
    for i in spots:
        sent.append(send(DB.at[z], DB.at[z], ds_sem.at[i], dr_sem.at[z], ring(i)))

    def outside(ref, *at):
        hollow = jnp.zeros((HALO, rows, LANES), F32)

        @pl.when(g == 0)
        def _():
            ref[(*at, pl.ds(0, HALO), body_rows)] = hollow

        @pl.when(g == tiles - 1)
        def _():
            ref[(*at, pl.ds(HALO + cols, HALO), body_rows)] = hollow

    def diffuse(f):
        landed(U.at[f, pl.ds(0, HALO), body_rows], hr_sem.at[0, f], left)
        landed(U.at[f, pl.ds(HALO + cols, HALO), body_rows], hr_sem.at[1, f], right)
        outside(U, f)
        for s in range(ITERS):
            src = U.at[f] if s == 0 else W.at[(s - 1) % 2]
            lo, n = s + 1, wide - 2 * (s + 1)
            lane = iota((n, 8, LANES), 2)
            acc = jnp.zeros((8, LANES), F32)
            for k in range(blocks):
                r = PAD + 8 * k
                cur = src[lo : lo + n, r : r + 8]
                below = src[lo : lo + n, r - 4 : r + 4]
                above = src[lo : lo + n, r + 4 : r + 12]
                south = pltpu.roll(jnp.where(lane == LANES - 1, below, cur), 1, 2)
                north_of = pltpu.roll(jnp.where(lane == 0, above, cur), LANES - 1, 2)
                around = (src[lo - 1 : lo - 1 + n, r : r + 8] + src[lo + 1 : lo + 1 + n, r : r + 8]) + (
                    south + north_of
                )
                new = (1.0 - 4.0 * DIFFUSION) * cur + DIFFUSION * around
                mine = new[HALO - lo : HALO - lo + cols]
                if s + 1 < ITERS:
                    W[s % 2, lo : lo + n, r : r + 8] = new
                else:
                    O[f, :, 8 * k : 8 * k + 8] = mine
                gap = D[f, :, 8 * k : 8 * k + 8] - mine
                acc = acc + jnp.sum(gap * gap, axis=0)
            if s + 1 < ITERS:
                outside(W, s % 2)
            ACC[s * fields + f] = acc

    early = fields - 1
    lax.fori_loop(0, early, lambda f, c: (diffuse(f), c)[1], 0)

    for i in spots:
        landed(QB.at[i], qr_sem.at[i], ring(i))
    q_sum = QB[0]
    for i in range(1, RING):
        q_sum = q_sum + QB[i]
    QC[me] = q_sum
    for i in others:
        sent.append(send(QC.at[me], QC.at[me], cs_sem.at[i], cr_sem.at[me], member(i)))

    lax.fori_loop(early, fields, lambda f, c: (diffuse(f), c)[1], 0)
    local = jnp.zeros((16, LANES), F32)
    for i in range(ITERS * fields):
        local = jnp.where(row16 == i, jnp.sum(ACC[i], axis=0, keepdims=True), local)
    SB[z] = local
    for i in spots:
        sent.append(send(SB.at[z], SB.at[z], ss_sem.at[i], sr_sem.at[z], ring(i)))

    for i in spots:
        landed(DB.at[i], dr_sem.at[i], ring(i))
    d_sum = DB[0]
    for i in range(1, RING):
        d_sum = d_sum + DB[i]
    ones, none = jnp.ones_like(d_sum), jnp.zeros_like(d_sum)
    from_r = substeps(ones, none)[-1][0]
    from_d = substeps(none, d_sum)[-1][0]
    r_sum = (q_sum - from_d) / from_r
    energy = jnp.zeros((16, LANES), F32)
    weight = -0.25 * (east + 1.0) * (north + 1.0)
    mine16 = jnp.where(upper, f_low + 1, f_low)
    for s, (t, r, v) in enumerate(substeps(r_sum, d_sum)):
        part = jnp.sum(weight * t * (r + v), axis=0, keepdims=True)
        energy = jnp.where(row16 == s * fields + mine16, part, energy)

    for i in others:
        landed(QC.at[i], cr_sem.at[i], member(i))
    for h in range(fields // 2):
        parts = []
        for l in range(levels):
            packed = QC[h * levels + l]
            parts += [packed, pltpu.roll(packed, 64, 1)]
        modal = jnp.dot(
            to_grid, jnp.concatenate(parts, axis=0), precision=HIGHEST, preferred_element_type=F32
        )
        for k in range(2):
            mine = jnp.where(lane_g // 32 == k, modal, 0.0)
            mine = mine + pltpu.roll(mine, 32, 1)
            mine = mine + pltpu.roll(mine, 64, 1)
            high = mine.astype(jnp.bfloat16).astype(F32)
            mine = jnp.where(lane_g < 64, high, mine - high)
            PS[2 * h + k] = jnp.concatenate(
                [jnp.where(odd_chunk, 0.0, mine), jnp.where(odd_chunk, mine, 0.0)], axis=1
            ).astype(jnp.bfloat16)
    for k in range(0, blocks, 2):
        quad = [T[:, pl.ds((2 * k + i) * LANES, LANES)] for i in range(4)]
        table = jnp.concatenate(
            [jnp.concatenate(quad[0::2], axis=1), jnp.concatenate(quad[1::2], axis=1)], axis=0
        )
        for f in range(fields):
            tend = jnp.dot(PS[f], table, preferred_element_type=F32)
            for i in range(2):
                at = pl.ds(8 * (k + i), 8)
                O[f, :, at] = O[f, :, at] + tend[:, i * LANES : (i + 1) * LANES].reshape(cols, 8, LANES)
        for t in range(2 * k, 2 * k + 4):
            pltpu.make_async_copy(
                o_view.at[:, :, t], o_hbm.at[:, :, :, pl.ds(t * LANES, LANES)], out_sem
            ).start()

    for i in spots:
        landed(SB.at[i], sr_sem.at[i], ring(i))
    sums = SB[0]
    for i in range(1, RING):
        sums = sums + SB[i]
    EB[me] = sums + energy
    for i in others:
        sent.append(send(EB.at[me], EB.at[me], es_sem.at[i], er_sem.at[me], member(i)))
    for i in others:
        landed(EB.at[i], er_sem.at[i], member(i))
    sums = EB[0]
    for i in range(1, members):
        sums = sums + EB[i]
    cells = float(levels * east * north)
    value = jnp.sqrt(jnp.maximum(jnp.sum(sums, axis=1, keepdims=True) / cells, 0.0))
    spread = jnp.where(row16 % fields == lane16, value, 0.0)
    row8 = iota((8, LANES), 0)
    log = jnp.zeros((8, LANES), F32)
    for s in range(ITERS):
        line = jnp.sum(spread[s * fields : (s + 1) * fields], axis=0, keepdims=True)
        log = jnp.where(row8 == s, line, log)
    res_ref[...] = log[:ITERS, :fields]

    for copy in sent:
        copy.wait_send()
    pltpu.make_async_copy(O, O, out_sem).wait()


def solution(mesh):
    tiles = mesh.shape["gx"]
    members = tiles // RING

    def local(model_state, driving, mode_east, mode_north, level_class, nudge_table):
        fields, levels, cols, north = model_state.shape
        rows = levels * north // LANES
        wide, high_rows = cols + 2 * HALO, rows + 2 * PAD
        vm = lambda *shape: pltpu.VMEM(shape, F32)
        dma = lambda *shape: pltpu.SemaphoreType.DMA(shape)
        smem = pl.BlockSpec(memory_space=pltpu.SMEM)
        anyw = pl.BlockSpec(memory_space=pl.ANY)
        scratch = [
            vm(fields, wide, high_rows, LANES), vm(fields, cols, rows, LANES), vm(fields, cols, rows, LANES),
            vm(2, wide, high_rows, LANES), pltpu.VMEM((LANES, north), jnp.bfloat16),
            vm(members, 32, LANES), vm(members, 32, LANES),
            vm(RING, 16, LANES), vm(RING, 16, LANES), vm(members, 16, LANES),
            vm(RING, 16, LANES), vm(members, 16, LANES),
            vm(ITERS * fields, 8, LANES), pltpu.VMEM((fields, 8 * cols, 2 * LANES), jnp.bfloat16),
            dma(2, fields), pltpu.SemaphoreType.DMA, dma(2, fields), dma(2, fields),
            dma(members), dma(members), dma(RING), dma(RING), dma(RING), dma(RING),
            dma(members), dma(members), dma(RING), dma(RING), dma(members), dma(members),
        ]
        turn = (0, 2, 1, 3)
        nudged, log = pl.pallas_call(
            functools.partial(kernel, tiles),
            out_shape=(
                jax.ShapeDtypeStruct((fields, cols, levels, north), F32),
                jax.ShapeDtypeStruct((ITERS, fields), F32),
            ),
            in_specs=[anyw, anyw, smem, smem, smem, smem],
            out_specs=(anyw, pl.BlockSpec(memory_space=pltpu.VMEM)),
            scratch_shapes=scratch,
            compiler_params=pltpu.CompilerParams(collective_id=0, has_side_effects=True),
        )(
            model_state.transpose(turn), driving.transpose(turn),
            mode_east, mode_north, level_class, nudge_table,
        )
        return nudged.transpose(turn), log

    tile = P("ens", None, "gx", None)
    return jax.shard_map(
        local, mesh=mesh, in_specs=(tile, tile, P(), P(), P(), P()),
        out_specs=(tile, P("ens", None)), check_vma=False,
    )
```

time: 502 us -> 74.3 us (0.15); the launches traced: 494 us -> 74.1 us
  blocking collectives: 368 us -> 0 us
  matrix products: 69.6 us -> 0 us
  Pallas kernels: 0 us -> 67.6 us
  starting transfers between devices: 24.5 us -> 0 us
  local copies, waits for them, and re-layouts: 20.5 us -> 5.9 us
  other arithmetic: 10.1 us -> 0 us
    psum x15 -> x0, blocking collectives: 368 us -> none  [by_axis(): value = lax.psum(value, axis)]
    dot_general x17 -> x0, matrix products: 69.6 us -> none  [the longest x4 42.6 us: local(): jnp.dot(partial_value.reshape(-1, partial_value.shape[-1]), table_north,...]
    pallas_call x0 -> x1, Pallas kernels: none -> 67.6 us  [local(): pl.pallas_call(functools.partial(kernel, tiles), out_shape=(jax.ShapeDtyp...]
    ppermute x2 -> x0, starting transfers between devices: 24.5 us -> none  [the longest x1 18.8 us: extended_2(): lax.ppermute(head, axis, [((i + 1) % count, i) for i in range(ends)])]
    slice x5 -> x0, local copies, waits for them, and re-layouts: 9.5 us -> none  [the longest x4 8.25 us: local(): extended[:, :, 1:-1]]
    unnamed x24 -> x5, local copies, waits for them, and re-layouts: 10.2 us -> 5.9 us
  transfers between devices with their start and end apart: 2 -> 0, of which waited for: 0 -> 0; matrix products, arithmetic and copies ran while one was open for 3% -> 0% of each run, Pallas kernels for 0% -> 0%
where the time goes in v1:
time: 74.3 us; the launch traced here: 74.1 us
  Pallas kernels  67.6 us (91%)
  local copies, waits for them, and re-layouts  5.9 us (8%)
    pallas_call x1, Pallas kernels, local(): pl.pallas_call(functools.partial(kernel, tiles), out_shape=(jax.ShapeDtyp...  67.6 us
    unnamed x5, local copies, waits for them, and re-layouts  5.9 us

profile of v1, /device:TPU:33, one launch (start us, length us, event | category | flops | bytes accessed | tf_op | source)
XLA Modules:
  0.0 74.1 jit_solution(17926007004026631621)
XLA Ops:
  0.6 1.3 %copy.8.nt_ref = f32[8,4]{1,0:T(8,128)} copy(f32[8,4]{0,1:T(4,128)} %param.11) | data formatting | bytes 256 | tf_op args[5]
  2.0 67.6 %shard_map.77 = (f32[4,20,4,2560]{3,2,1,0:T(4,128)}, f32[4,4]{1,0:T(4,128)}) custom-call(f32[4,20,4,2560]{3,2,1,0:T(4,128)} %bitcast.3, f32[4,20,4,2560]{3,2,1,0:T(4,128)} %bitcast.4, s32[30]{0:T(128)} %me_ref.1, s32[30]{0:T(128)} %mn_ref.1, s32[4]{0:T(128)} %lc_ref.1, f32[8,4]{1,0:T(8,128)} %copy.8.nt_ref), custom_call_target="tpu_custom_call" | custom-call | tf_op jit(solution)/shard_map/pallas_call | solution.py:424
  69.5 0.0 copy-start
  69.6 4.0 %copy.11 = f32[4,4,20,2560]{3,1,2,0:T(4,128)} copy(f32[4,4,20,2560]{3,1,2,0:T(4,128)} %bitcast.5) | data formatting | bytes 6553600
  73.5 0.0 copy-done
  73.5 0.6 copy.12
Async XLA Ops:
  69.5 4.0 %copy-start = (f32[4,4]{1,0:T(4,128)S(1)}, f32[4,4]{1,0:T(4,128)}, u32[]{:S(2)}) copy-start(f32[4,4]{1,0:T(4,128)} %get-tuple-element.9) | copy-start | bytes 196

commit v2 on v1

v2 whole, which is shorter than its diff:
```python
import functools

import jax
import jax.numpy as jnp
import numpy as np
from jax import lax
from jax.experimental import pallas as pl
from jax.experimental.pallas import tpu as pltpu
from jax.sharding import PartitionSpec as P

ITERS = 4
DIFFUSION = 0.24
CORES = 2
RING = 16
MESH = pl.DeviceIdType.MESH
HIGHEST = lax.Precision.HIGHEST
F32 = jnp.float32
LANES = 128
HALO = 4
PAD = 8
STRIPS = 4


def iota(shape, dim):
    return lax.broadcasted_iota(jnp.int32, shape, dim)


def pick(ref, which, count):
    out = jnp.zeros(which.shape, F32)
    for i in range(count):
        out = jnp.where(which == i, ref[i].astype(F32), out)
    return out


def sine(product, period):
    turns = jnp.floor(product * (1.0 / period) + 0.5)
    x = (product - turns * period) * (np.pi / period)
    odd = turns - 2.0 * jnp.floor(turns * 0.5)
    y = x * x
    poly = 1.0 / 6227020800.0
    for c in (-1.0 / 39916800.0, 1.0 / 362880.0, -1.0 / 5040.0, 1.0 / 120.0, -1.0 / 6.0, 1.0):
        poly = poly * y + c
    return x * poly * (1.0 - 2.0 * odd)


def split(value):
    high = value.astype(jnp.bfloat16)
    return high, (value - high.astype(F32)).astype(jnp.bfloat16)


def kernel(
    tiles, u_hbm, d_hbm, me_hbm, mn_hbm, lc_hbm, nt_hbm, O, log_ref,
    me_ref, mn_ref, lc_ref, nt_ref, U, D, W, T, CA, RA, QB, XP, XB, QC, SB, EB, ACC, PS,
    small_sem, in_sem, edge_sem, sems,
):
    fields, cols, levels, north = u_hbm.shape
    kx, ky = me_ref.shape[0], mn_ref.shape[0]
    east = cols * tiles
    members = tiles // RING
    chunks = north // LANES
    blocks = chunks // 2
    wide = cols + 2 * HALO
    rows = 8 * blocks
    high_rows = rows + 2 * PAD
    own = pl.ds(HALO, cols)
    g = lax.axis_index("gx")
    core = lax.rem(g, CORES)
    z = lax.rem(g // CORES, RING)
    xi = g // (CORES * RING)
    me = xi * CORES + core

    def member(i):
        return {"gx": ((i // CORES) * RING + z) * CORES + lax.rem(i, CORES)}

    def ring(i):
        return {"gx": (xi * RING + i) * CORES + core}

    right = {"gx": lax.rem(g + 1, tiles)}
    left = {"gx": lax.rem(g + tiles - 1, tiles)}
    others = [lax.rem(me + k, members) for k in range(1, members)]
    far_first = sorted(range(1, RING), key=lambda k: -min(k, RING - k))
    spots = [lax.rem(z + k, RING) for k in far_first]

    u_view = U.reshape(fields, wide, high_rows // levels, levels, LANES)
    d_view = D.reshape(fields, cols, chunks, levels, LANES)
    skip = PAD // levels
    small = []
    for i, (hbm, ref) in enumerate(((me_hbm, me_ref), (mn_hbm, mn_ref), (lc_hbm, lc_ref), (nt_hbm, nt_ref))):
        small.append(pltpu.make_async_copy(hbm, ref, small_sem.at[i]))
        small[-1].start()
    for h in range(0, fields, 2):
        two = pl.ds(h, 2)
        for i in range(2):
            for t in range(chunks):
                hbm, dst = (
                    (u_hbm, u_view.at[two, own, skip + t]) if i == 0 else (d_hbm, d_view.at[two, :, t])
                )
                pltpu.make_async_copy(
                    hbm.at[two, :, :, pl.ds(t * LANES, LANES)], dst, in_sem.at[i, h // 2]
                ).start()

    def loaded(i, h):
        two = pl.ds(h, 2)
        ref = U.at[two, own, pl.ds(PAD, rows)] if i == 0 else D.at[two]
        pltpu.make_async_copy(ref, ref, in_sem.at[i, h // 2]).wait()

    barrier = pltpu.get_barrier_semaphore()
    greeted = [member(i) for i in others] + [ring(i) for i in spots] + [left, right]
    for who in greeted:
        pl.semaphore_signal(barrier, inc=1, device_id=who, device_id_type=MESH)

    for copy in small:
        copy.wait()
    row32 = iota((32, LANES), 0)
    lane32 = iota((32, LANES), 1)
    modes_n = pick(mn_ref, row32, ky)
    for c in range(chunks):
        place = (lane32 + (c * LANES + 1)).astype(F32)
        high, low = split(sine(modes_n * place, float(north + 1)))
        at = pl.ds(c * LANES, LANES)
        both = jnp.concatenate([high, low], axis=0)
        T[0:64, at] = both
        T[64:128, at] = both
    first = g * cols
    count = 8 * cols
    grid_rows = 8 * ((count + LANES - 1) // LANES) * (LANES // 8)
    row_m, lane_m = iota((LANES, grid_rows), 0), iota((LANES, grid_rows), 1)
    mode_m = pick(me_ref, iota((LANES, LANES), 0) % 32, kx)
    mode_m = jnp.concatenate([mode_m] * (grid_rows // LANES), axis=1)
    to_modes = jnp.where(
        (lane_m < count) & (row_m // 32 == lane_m % 4),
        sine(mode_m * (lane_m // 8 + first + 1).astype(F32), float(east + 1)), 0.0,
    )
    row_g, lane_g = iota((count, LANES), 0), iota((count, LANES), 1)
    mode_g = jnp.concatenate([pick(me_ref, iota((8, LANES), 1) % 32, kx)] * cols, axis=0)
    to_grid = jnp.where(
        row_g % 4 == lane_g // 32,
        sine(mode_g * (row_g // 8 + first + 1).astype(F32), float(east + 1)), 0.0,
    )
    edge = jnp.zeros((wide, PAD, LANES), F32)
    for f in range(fields):
        U[f, :, 0:PAD] = edge
        U[f, :, PAD + rows : high_rows] = edge
    for s in range(2):
        W[s, :, 0:PAD] = edge
        W[s, :, PAD + rows : high_rows] = edge

    row16 = iota((16, LANES), 0)
    lane16 = iota((16, LANES), 1)
    f_low = 2 * (me // levels)
    my_class = lc_ref[lax.rem(me, levels)]
    w_low, w_up = nt_ref[f_low, my_class], nt_ref[f_low + 1, my_class]
    share = 16 // RING

    def constants(top, count):
        lane = iota((count, LANES), 1)
        a = iota((count, LANES), 0) + top + jnp.where(lane >= 64, 16, 0)
        half_e = sine(pick(me_ref, a, kx), 2.0 * (east + 1))
        half_n = sine(pick(mn_ref, lane % 32, ky), 2.0 * (north + 1))
        fade = (4.0 * DIFFUSION) * (half_e * half_e + half_n * half_n)
        return fade, jnp.where(lane % 64 >= 32, w_up, w_low)

    def substeps(fade, w, r, d):
        lam = 1.0 - fade
        t = jnp.zeros_like(r)
        v = r
        out = []
        for _ in range(ITERS):
            t = lam * t + w * r
            r = (lam - w) * r + fade * d
            v = lam * v + fade * d
            out.append((t, r, v))
        return out

    all_modes = constants(0, 16)
    my_modes = constants(z * share, share)

    norm = 4.0 / ((east + 1) * (north + 1))
    odd_chunk = row_g % 8 >= 4
    contract_lanes = (((1,), (1,)), ((), ()))
    for h in range(0, fields, 2):
        loaded(0, h)
        loaded(1, h)
        acc_r = acc_d = None
        held = []
        for k in range(blocks):
            at = pl.ds(8 * k, 8)
            d = D[h : h + 2, :, at]
            r = d - U[h : h + 2, own, pl.ds(PAD + 8 * k, 8)]
            high, low = split(r.reshape(2 * count, LANES))
            table = jnp.concatenate(
                [T[0:64, pl.ds((2 * k + p) * LANES, LANES)] for p in range(2)], axis=0
            )
            out = lax.dot_general(
                jnp.concatenate([high, low], axis=1), jnp.concatenate([table, table], axis=1),
                contract_lanes, preferred_element_type=F32,
            )
            acc_r = out if acc_r is None else acc_r + out
            held.append((d.reshape(2 * count, LANES).astype(jnp.bfloat16), table))
            if len(held) == 2:
                out = lax.dot_general(
                    jnp.concatenate([held[0][0], held[1][0]], axis=1),
                    jnp.concatenate([held[0][1], held[1][1]], axis=1),
                    contract_lanes, preferred_element_type=F32,
                )
                acc_d = out if acc_d is None else acc_d + out
                held = []
        mix = jnp.zeros((count, LANES), F32)
        for i, acc in enumerate((acc_r, acc_d)):
            acc = acc + pltpu.roll(acc, 32, 1)
            for j in range(2):
                mine = acc[j * count : (j + 1) * count]
                slot = 2 * i + j
                even, odd = ((slot - 1) % 4) * 32, ((slot + 1) % 4) * 32
                even = pltpu.roll(mine, even, 1) if even else mine
                odd = pltpu.roll(mine, odd, 1) if odd else mine
                mix = jnp.where(lane_g // 32 == slot, jnp.where(odd_chunk, odd, even), mix)
        if grid_rows > count:
            mix = jnp.concatenate([mix, jnp.zeros((grid_rows - count, LANES), F32)], axis=0)
        modal = norm * jnp.dot(to_modes, mix, precision=HIGHEST, preferred_element_type=F32)
        for l in range(levels):
            CA[(h // 2) * levels + l] = modal[32 * l : 32 * l + 32]

    pl.semaphore_wait(barrier, len(greeted))

    def send(src, dst, phase, who, recv_sem=None):
        pltpu.make_async_remote_copy(
            src_ref=src, dst_ref=dst, send_sem=sems.at[0, phase],
            recv_sem=sems.at[1, phase] if recv_sem is None else recv_sem,
            device_id=who, device_id_type=MESH,
        ).start()

    def both_ends(ref, phase, recv_sem=None):
        return pltpu.make_async_remote_copy(
            src_ref=ref, dst_ref=ref, send_sem=sems.at[0, phase],
            recv_sem=sems.at[1, phase] if recv_sem is None else recv_sem,
            device_id=right, device_id_type=MESH,
        )

    EDGE, SLICE, SHARE, SUM, BACK, PART, LOG = range(7)
    body_rows = pl.ds(PAD, rows)
    west, inner_west = pl.ds(0, HALO), pl.ds(HALO, HALO)
    inner_east, east_edge = pl.ds(cols, HALO), pl.ds(HALO + cols, HALO)

    def send_edges(f):
        send(U.at[f, inner_east, body_rows], U.at[f, west, body_rows], EDGE, right, edge_sem.at[0, f])
        send(U.at[f, inner_west, body_rows], U.at[f, east_edge, body_rows], EDGE, left, edge_sem.at[1, f])

    send_edges(0)
    for i in others:
        send(CA.at[i], RA.at[me], SLICE, member(i))
    for f in range(1, fields):
        send_edges(f)
    RA[me] = CA[me]

    def outside(ref, *at):
        hollow = jnp.zeros((HALO, rows, LANES), F32)

        @pl.when(g == 0)
        def _():
            ref[(*at, pl.ds(0, HALO), body_rows)] = hollow

        @pl.when(g == tiles - 1)
        def _():
            ref[(*at, pl.ds(HALO + cols, HALO), body_rows)] = hollow

    def diffuse(f):
        both_ends(U.at[f, west, body_rows], EDGE, edge_sem.at[0, f]).wait_recv()
        both_ends(U.at[f, east_edge, body_rows], EDGE, edge_sem.at[1, f]).wait_recv()
        outside(U, f)
        for s in range(ITERS):
            src = U.at[f] if s == 0 else W.at[(s - 1) % 2]
            lo, hi = s + 1, wide - (s + 1)
            cuts = [lo + (hi - lo) * i // STRIPS for i in range(STRIPS + 1)]
            acc = jnp.zeros((8, LANES), F32)
            for k in range(blocks):
                r = PAD + 8 * k
                for x0, x1 in zip(cuts[:-1], cuts[1:]):
                    near = src[x0 - 1 : x1 + 1, r : r + 8]
                    cur = near[1:-1]
                    lane = iota((x1 - x0, 8, LANES), 2)
                    below = src[x0:x1, r - 4 : r + 4]
                    above = src[x0:x1, r + 4 : r + 12]
                    south = pltpu.roll(jnp.where(lane == LANES - 1, below, cur), 1, 2)
                    north_of = pltpu.roll(jnp.where(lane == 0, above, cur), LANES - 1, 2)
                    around = (near[:-2] + near[2:]) + (south + north_of)
                    new = (1.0 - 4.0 * DIFFUSION) * cur + DIFFUSION * around
                    if s + 1 < ITERS:
                        W[s % 2, x0:x1, r : r + 8] = new
                    y0, y1 = max(x0, HALO), min(x1, HALO + cols)
                    if y0 >= y1:
                        continue
                    at = slice(y0 - HALO, y1 - HALO)
                    new = new[y0 - x0 : y1 - x0]
                    if s + 1 == ITERS:
                        O[f, at, 8 * k : 8 * k + 8] = new
                    gap = D[f, at, 8 * k : 8 * k + 8] - new
                    acc = acc + jnp.sum(gap * gap, axis=0)
            if s + 1 < ITERS:
                outside(W, s % 2)
            ACC[s * fields + f] = acc

    diffuse(0)
    both_ends(RA.at[pl.ds(0, members - 1)], SLICE).wait_recv()
    total = RA[0]
    for i in range(1, members):
        total = total + RA[i]
    turned = pltpu.roll(total, 64, 1)
    left_half = lane16 < 64
    r_part = jnp.where(left_half, total[0:16], turned[16:32])
    d_part = jnp.where(left_half, turned[0:16], total[16:32])
    for i in range(RING):
        part = slice(i * share, (i + 1) * share)
        XP[i] = jnp.concatenate([r_part[part], d_part[part]], axis=0)
    for i in spots:
        send(XP.at[i], XB.at[z], SHARE, ring(i))
    QB[z] = substeps(*all_modes, r_part, d_part)[-1][0]
    for i in spots:
        send(QB.at[z], QB.at[z], SUM, ring(i))
    XB[z] = XP[z]
    lax.fori_loop(1, fields, lambda f, c: (diffuse(f), c)[1], 0)

    both_ends(XB.at[pl.ds(0, RING - 1)], SHARE).wait_recv()
    shares = XB[0]
    for i in range(1, RING):
        shares = shares + XB[i]
    r_sum, d_sum = shares[:share], shares[share:]
    energy = jnp.zeros((16, LANES), F32)
    weight = -0.25 * (east + 1.0) * (north + 1.0)
    my_field = jnp.where(lane16 % 64 >= 32, f_low + 1, f_low)
    for s, (t, r, v) in enumerate(substeps(*my_modes, r_sum, d_sum)):
        part = jnp.sum(weight * t * (r + v), axis=0, keepdims=True)
        energy = jnp.where(row16 == s * fields + my_field, part, energy)
    for i in range(ITERS * fields):
        energy = energy + jnp.where(row16 == i, jnp.sum(ACC[i], axis=0, keepdims=True), 0.0)
    energy = jnp.sum(energy, axis=1, keepdims=True)
    SB[z] = jnp.sum(jnp.where(row16 == lane16, energy, 0.0), axis=0, keepdims=True)
    for i in spots:
        send(SB.at[z], SB.at[z], PART, ring(i))

    both_ends(QB.at[pl.ds(0, RING - 1)], SUM).wait_recv()
    q_sum = QB[0]
    for i in range(1, RING):
        q_sum = q_sum + QB[i]
    QC[me] = q_sum
    for i in others:
        send(QC.at[me], QC.at[me], BACK, member(i))

    both_ends(QC.at[pl.ds(0, members - 1)], BACK).wait_recv()
    for h in range(fields // 2):
        parts = []
        for l in range(levels):
            packed = QC[h * levels + l]
            parts += [packed, pltpu.roll(packed, 64, 1)]
        modal = jnp.dot(
            to_grid, jnp.concatenate(parts, axis=0), precision=HIGHEST, preferred_element_type=F32
        )
        for k in range(2):
            mine = jnp.where(lane_g // 32 == k, modal, 0.0)
            mine = mine + pltpu.roll(mine, 32, 1)
            mine = mine + pltpu.roll(mine, 64, 1)
            high = mine.astype(jnp.bfloat16).astype(F32)
            mine = jnp.where(lane_g < 64, high, mine - high)
            PS[2 * h + k] = jnp.concatenate(
                [jnp.where(odd_chunk, 0.0, mine), jnp.where(odd_chunk, mine, 0.0)], axis=1
            ).astype(jnp.bfloat16)
    for k in range(0, blocks, 2):
        quad = [T[:, pl.ds((2 * k + i) * LANES, LANES)] for i in range(4)]
        table = jnp.concatenate(
            [jnp.concatenate(quad[0::2], axis=1), jnp.concatenate(quad[1::2], axis=1)], axis=0
        )
        for f in range(fields):
            tend = jnp.dot(PS[f], table, preferred_element_type=F32)
            for i in range(2):
                at = pl.ds(8 * (k + i), 8)
                O[f, :, at] = O[f, :, at] + tend[:, i * LANES : (i + 1) * LANES].reshape(cols, 8, LANES)

    both_ends(SB.at[pl.ds(0, RING - 1)], PART).wait_recv()
    sums = SB[0]
    for i in range(1, RING):
        sums = sums + SB[i]
    EB[me] = sums
    for i in others:
        send(EB.at[me], EB.at[me], LOG, member(i))
    both_ends(EB.at[pl.ds(0, members - 1)], LOG).wait_recv()
    sums = EB[0]
    for i in range(1, members):
        sums = sums + EB[i]
    cells = float(levels * east * north)
    value = jnp.broadcast_to(jnp.sqrt(jnp.maximum(sums / cells, 0.0)), (8, LANES))
    row8 = iota((8, LANES), 0)
    log = value
    for s in range(1, ITERS):
        log = jnp.where(row8 == s, pltpu.roll(value, LANES - s * fields, 1), log)
    log_ref[...] = log

    both_ends(U.at[:, pl.ds(0, 2 * HALO), body_rows], EDGE).wait_send()
    for phase, buf in ((SLICE, RA), (SHARE, XB), (SUM, QB), (BACK, QC), (PART, SB), (LOG, EB)):
        both_ends(buf.at[pl.ds(0, buf.shape[0] - 1)], phase).wait_send()


def writer(O, log_ref, o_hbm, res_ref, sem):
    fields, cols, levels, north = o_hbm.shape
    chunks = north // LANES
    o_view = O.reshape(fields, cols, chunks, levels, LANES)
    for t in range(chunks):
        pltpu.make_async_copy(
            o_view.at[:, :, t], o_hbm.at[:, :, :, pl.ds(t * LANES, LANES)], sem
        ).start()
    res_ref[...] = log_ref[: res_ref.shape[0], : res_ref.shape[1]]
    pltpu.make_async_copy(O, O, sem).wait()


def solution(mesh):
    tiles = mesh.shape["gx"]
    members = tiles // RING

    def local(model_state, driving, mode_east, mode_north, level_class, nudge_table):
        fields, levels, cols, north = model_state.shape
        rows = levels * north // LANES
        wide, high_rows = cols + 2 * HALO, rows + 2 * PAD
        share = 16 // RING
        vm = lambda *shape: pltpu.VMEM(shape, F32)
        dma = lambda *shape: pltpu.SemaphoreType.DMA(shape)
        hbm = pl.BlockSpec(memory_space=pltpu.HBM)
        smem = lambda ref: pltpu.SMEM(ref.shape, ref.dtype)
        table = nudge_table.T
        scratch = [
            smem(mode_east), smem(mode_north), smem(level_class), smem(table),
            vm(fields, wide, high_rows, LANES), vm(fields, cols, rows, LANES),
            vm(2, wide, high_rows, LANES), pltpu.VMEM((LANES, north), jnp.bfloat16),
            vm(members, 32, LANES), vm(members, 32, LANES),
            vm(RING, 16, LANES), vm(RING, 2 * share, LANES), vm(RING, 2 * share, LANES), vm(members, 16, LANES),
            vm(RING, 1, LANES), vm(members, 1, LANES),
            vm(ITERS * fields, 8, LANES), pltpu.VMEM((fields, 8 * cols, 2 * LANES), jnp.bfloat16),
            dma(4), dma(2, fields // 2), dma(2, fields), dma(2, 7),
        ]
        turn = (0, 2, 1, 3)
        inner = pl.BlockSpec(memory_space=pltpu.VMEM)
        grid, log = pl.pallas_call(
            functools.partial(kernel, tiles),
            out_shape=(
                vm(fields, cols, rows, LANES),
                vm(8, LANES),
            ),
            in_specs=[hbm] * 6,
            out_specs=(inner, inner),
            scratch_shapes=scratch,
            compiler_params=pltpu.CompilerParams(
                collective_id=0, has_side_effects=True, vmem_limit_bytes=60 * 2**20
            ),
        )(
            model_state.transpose(turn), driving.transpose(turn),
            mode_east, mode_north, level_class, table,
        )
        nudged, log = pl.pallas_call(
            writer,
            out_shape=(
                jax.ShapeDtypeStruct((fields, cols, levels, north), F32),
                jax.ShapeDtypeStruct((ITERS, fields), F32),
            ),
            in_specs=[inner, inner],
            out_specs=(hbm, inner),
            scratch_shapes=[pltpu.SemaphoreType.DMA],
            compiler_params=pltpu.CompilerParams(vmem_limit_bytes=8 * 2**20),
        )(grid, log)
        return nudged.transpose(turn), log

    tile = P("ens", None, "gx", None)
    return jax.shard_map(
        local, mesh=mesh, in_specs=(tile, tile, P(), P(), P(), P()),
        out_specs=(tile, P("ens", None)), check_vma=False,
    )
```

time: 74.3 us -> 60.4 us (0.81)
  Pallas kernels: 67.6 us -> 59.7 us
  local copies, waits for them, and re-layouts: 5.9 us -> 0 us
    pallas_call x1 -> x2, Pallas kernels: 67.6 us -> 59.7 us  [the longest x1 57.4 us: local(): pl.pallas_call(functools.partial(kernel, tiles), out_shape=(vm(fields, co...]
    unnamed x5 -> x0, local copies, waits for them, and re-layouts: 5.9 us -> none
where the time goes in v2:
time: 60.4 us; the launch traced here: 60.3 us
  Pallas kernels  59.7 us (99%)
  between operations  0.64 us (1%)
    pallas_call x1, Pallas kernels, local(): pl.pallas_call(functools.partial(kernel, tiles), out_shape=(vm(fields, co...  57.4 us
    pallas_call x1, Pallas kernels, local(): pl.pallas_call(writer, out_shape=(jax.ShapeDtypeStruct((fields, cols, lev...  2.27 us

profile of v2, /device:TPU:33, one launch (start us, length us, event | category | flops | bytes accessed | tf_op | source)
XLA Modules:
  0.0 60.3 jit_solution(11103077034316433355)
XLA Ops:
  0.6 57.4 %shard_map.77 = (f32[4,20,80,128]{3,2,1,0:T(8,128)S(1)}, f32[8,128]{1,0:T(8,128)S(1)}) custom-call(f32[4,20,4,2560]{3,2,1,0:T(4,128)} %bitcast.4, f32[4,20,4,2560]{3,2,1,0:T(4,128)} %bitcast.5, s32[30]{0:T(128)} %me_hbm.1, s32[30]{0:T(128)} %mn_hbm.1, s32[4]{0:T(128)} %lc_hbm.1, f32[4,8]{1,0:T(4,128)} %bitcast.6), custom_call_target="tpu_custom_call" | custom-call | tf_op jit(solution)/shard_map/pallas_call | solution.py:440
  58.0 2.3 %shard_map.78 = (f32[4,20,4,2560]{3,2,1,0:T(4,128)}, f32[4,4]{1,0:T(4,128)}) custom-call(f32[4,20,80,128]{3,2,1,0:T(8,128)S(1)} %get-tuple-element.6.O, f32[8,128]{1,0:T(8,128)S(1)} %get-tuple-element.7.log_ref), custom_call_target="tpu_custom_call" | custom-call | tf_op jit(solution)/shard_map/pallas_call | solution.py:456

commit v3 on v2

--- a/solution.py
+++ b/solution.py
@@ -18,7 +18,8 @@
 LANES = 128
 HALO = 4
 PAD = 8
-STRIPS = 4
+INNER_STRIPS = 3
+AHEAD = 1
 
 
 def iota(shape, dim):
@@ -50,13 +51,14 @@
 
 def kernel(
     tiles, u_hbm, d_hbm, me_hbm, mn_hbm, lc_hbm, nt_hbm, O, log_ref,
-    me_ref, mn_ref, lc_ref, nt_ref, U, D, W, T, CA, RA, QB, XP, XB, QC, SB, EB, ACC, PS,
-    small_sem, in_sem, edge_sem, sems,
+    me_ref, mn_ref, lc_ref, nt_ref, U, D, W, T, XD, PX, XS, XB, Y, YP, QD, ACC, PS,
+    small_sem, in_sem, edge_sem, sems, heard,
 ):
     fields, cols, levels, north = u_hbm.shape
     kx, ky = me_ref.shape[0], mn_ref.shape[0]
     east = cols * tiles
-    members = tiles // RING
+    chips = tiles // CORES
+    share = 16 * levels // chips
     chunks = north // LANES
     blocks = chunks // 2
     wide = cols + 2 * HALO
@@ -67,19 +69,38 @@
     core = lax.rem(g, CORES)
     z = lax.rem(g // CORES, RING)
     xi = g // (CORES * RING)
-    me = xi * CORES + core
-
-    def member(i):
-        return {"gx": ((i // CORES) * RING + z) * CORES + lax.rem(i, CORES)}
-
-    def ring(i):
-        return {"gx": (xi * RING + i) * CORES + core}
-
+    chip = g // CORES
+    partner = {"gx": chip * CORES + (CORES - 1 - core)}
     right = {"gx": lax.rem(g + 1, tiles)}
     left = {"gx": lax.rem(g + tiles - 1, tiles)}
-    others = [lax.rem(me + k, members) for k in range(1, members)]
-    far_first = sorted(range(1, RING), key=lambda k: -min(k, RING - k))
-    spots = [lax.rem(z + k, RING) for k in far_first]
+    across = chips // RING
+    far_first = sorted(range(RING), key=lambda k: -min(k, RING - k))
+    z_spots = [lax.rem(z + k, RING) for k in far_first]
+    x_spots = [lax.rem(xi + k, across) * RING for k in range(across)]
+    others = [x_spots[i] + z_spots[k] for k in range(RING) for i in range(across)]
+    del others[RING * across - across]
+
+    def peer(i):
+        return {"gx": i * CORES + core}
+
+    barrier = pltpu.get_barrier_semaphore()
+    beside = [lax.rem(z + 1, RING), lax.rem(z + RING - 1, RING)]
+    greeted = [partner, left, right] + [peer(x_spots[i] + z) for i in range(1, across)]
+    greeted += [peer(x + there) for there in beside for x in x_spots]
+    for who in greeted:
+        pl.semaphore_signal(barrier, inc=1, device_id=who, device_id_type=MESH)
+    rounds = [1 << i for i in range(8) if 4 << i <= RING]
+
+    def hear(i):
+        if i < len(rounds):
+            pl.semaphore_wait(heard.at[i], 2)
+
+    def tell(i):
+        if i < len(rounds):
+            for there in (lax.rem(z + rounds[i], RING), lax.rem(z + RING - rounds[i], RING)):
+                pl.semaphore_signal(
+                    heard.at[i], inc=1, device_id=peer(xi * RING + there), device_id_type=MESH
+                )
 
     u_view = U.reshape(fields, wide, high_rows // levels, levels, LANES)
     d_view = D.reshape(fields, cols, chunks, levels, LANES)
@@ -103,11 +124,6 @@
         two = pl.ds(h, 2)
         ref = U.at[two, own, pl.ds(PAD, rows)] if i == 0 else D.at[two]
         pltpu.make_async_copy(ref, ref, in_sem.at[i, h // 2]).wait()
-
-    barrier = pltpu.get_barrier_semaphore()
-    greeted = [member(i) for i in others] + [ring(i) for i in spots] + [left, right]
-    for who in greeted:
-        pl.semaphore_signal(barrier, inc=1, device_id=who, device_id_type=MESH)
 
     for copy in small:
         copy.wait()
@@ -137,20 +153,11 @@
         row_g % 4 == lane_g // 32,
         sine(mode_g * (row_g // 8 + first + 1).astype(F32), float(east + 1)), 0.0,
     )
-    edge = jnp.zeros((wide, PAD, LANES), F32)
-    for f in range(fields):
-        U[f, :, 0:PAD] = edge
-        U[f, :, PAD + rows : high_rows] = edge
-    for s in range(2):
-        W[s, :, 0:PAD] = edge
-        W[s, :, PAD + rows : high_rows] = edge
-
     row16 = iota((16, LANES), 0)
     lane16 = iota((16, LANES), 1)
-    f_low = 2 * (me // levels)
-    my_class = lc_ref[lax.rem(me, levels)]
+    f_low = 2 * core
+    my_class = lc_ref[(chip * share) // 16]
     w_low, w_up = nt_ref[f_low, my_class], nt_ref[f_low + 1, my_class]
-    share = 16 // RING
 
     def constants(top, count):
         lane = iota((count, LANES), 1)
@@ -172,8 +179,33 @@
             out.append((t, r, v))
         return out
 
-    all_modes = constants(0, 16)
-    my_modes = constants(z * share, share)
+    my_modes = constants(lax.rem(chip * share, 16), share)
+
+    pl.semaphore_wait(barrier, len(greeted))
+    tell(0)
+
+    def send(src, dst, phase, who, recv_sem=None):
+        pltpu.make_async_remote_copy(
+            src_ref=src, dst_ref=dst, send_sem=sems.at[0, phase],
+            recv_sem=sems.at[1, phase] if recv_sem is None else recv_sem,
+            device_id=who, device_id_type=MESH,
+        ).start()
+
+    def both_ends(ref, phase, recv_sem=None):
+        return pltpu.make_async_remote_copy(
+            src_ref=ref, dst_ref=ref, send_sem=sems.at[0, phase],
+            recv_sem=sems.at[1, phase] if recv_sem is None else recv_sem,
+            device_id=right, device_id_type=MESH,
+        )
+
+    EDGE, PAIR, SHARE, ALL, BACK = range(5)
+    body_rows = pl.ds(PAD, rows)
+    west, inner_west = pl.ds(0, HALO), pl.ds(HALO, HALO)
+    inner_east, east_edge = pl.ds(cols, HALO), pl.ds(HALO + cols, HALO)
+
+    def send_edges(f):
+        send(U.at[f, inner_east, body_rows], U.at[f, west, body_rows], EDGE, right, edge_sem.at[0, f])
+        send(U.at[f, inner_west, body_rows], U.at[f, east_edge, body_rows], EDGE, left, edge_sem.at[1, f])
 
     norm = 4.0 / ((east + 1) * (north + 1))
     odd_chunk = row_g % 8 >= 4
@@ -218,40 +250,15 @@
         if grid_rows > count:
             mix = jnp.concatenate([mix, jnp.zeros((grid_rows - count, LANES), F32)], axis=0)
         modal = norm * jnp.dot(to_modes, mix, precision=HIGHEST, preferred_element_type=F32)
+        turned = pltpu.roll(modal, 64, 1)
+        send_edges(h)
+        send_edges(h + 1)
+        hear(h // 2)
+        tell(h // 2 + 1)
         for l in range(levels):
-            CA[(h // 2) * levels + l] = modal[32 * l : 32 * l + 32]
-
-    pl.semaphore_wait(barrier, len(greeted))
-
-    def send(src, dst, phase, who, recv_sem=None):
-        pltpu.make_async_remote_copy(
-            src_ref=src, dst_ref=dst, send_sem=sems.at[0, phase],
-            recv_sem=sems.at[1, phase] if recv_sem is None else recv_sem,
-            device_id=who, device_id_type=MESH,
-        ).start()
-
-    def both_ends(ref, phase, recv_sem=None):
-        return pltpu.make_async_remote_copy(
-            src_ref=ref, dst_ref=ref, send_sem=sems.at[0, phase],
-            recv_sem=sems.at[1, phase] if recv_sem is None else recv_sem,
-            device_id=right, device_id_type=MESH,
-        )
-
-    EDGE, SLICE, SHARE, SUM, BACK, PART, LOG = range(7)
-    body_rows = pl.ds(PAD, rows)
-    west, inner_west = pl.ds(0, HALO), pl.ds(HALO, HALO)
-    inner_east, east_edge = pl.ds(cols, HALO), pl.ds(HALO + cols, HALO)
-
-    def send_edges(f):
-        send(U.at[f, inner_east, body_rows], U.at[f, west, body_rows], EDGE, right, edge_sem.at[0, f])
-        send(U.at[f, inner_west, body_rows], U.at[f, east_edge, body_rows], EDGE, left, edge_sem.at[1, f])
-
-    send_edges(0)
-    for i in others:
-        send(CA.at[i], RA.at[me], SLICE, member(i))
-    for f in range(1, fields):
-        send_edges(f)
-    RA[me] = CA[me]
+            upper_a, lower_a = slice(32 * l, 32 * l + 16), slice(32 * l + 16, 32 * l + 32)
+            XD[h // 2, 32 * l : 32 * l + 16] = jnp.where(lane16 < 64, modal[upper_a], turned[lower_a])
+            XD[h // 2, 32 * l + 16 : 32 * l + 32] = jnp.where(lane16 < 64, turned[upper_a], modal[lower_a])
 
     def outside(ref, *at):
         hollow = jnp.zeros((HALO, rows, LANES), F32)
@@ -264,93 +271,103 @@
         def _():
             ref[(*at, pl.ds(HALO + cols, HALO), body_rows)] = hollow
 
-    def diffuse(f):
+    def update(f, s, bounds, strips):
+        src = U.at[f] if s == 0 else W.at[f, s - 1]
+        acc = jnp.zeros((8, LANES), F32)
+        cuts = []
+        for lo, hi in bounds:
+            cuts += [(lo + (hi - lo) * i // strips, lo + (hi - lo) * (i + 1) // strips) for i in range(strips)]
+        for k in range(blocks):
+            r = PAD + 8 * k
+            for x0, x1 in cuts:
+                near = src[x0 - 1 : x1 + 1, r : r + 8]
+                cur = near[1:-1]
+                lane = iota((x1 - x0, 8, LANES), 2)
+                below = src[x0:x1, r - 4 : r + 4]
+                above = src[x0:x1, r + 4 : r + 12]
+                south = pltpu.roll(jnp.where(lane == LANES - 1, below, cur), 1, 2)
+                north_of = pltpu.roll(jnp.where(lane == 0, above, cur), LANES - 1, 2)
+                around = (near[:-2] + near[2:]) + (south + north_of)
+                new = (1.0 - 4.0 * DIFFUSION) * cur + DIFFUSION * around
+                if s + 1 < ITERS:
+                    W[f, s, x0:x1, r : r + 8] = new
+                y0, y1 = max(x0, HALO), min(x1, HALO + cols)
+                if y0 >= y1:
+                    continue
+                at = slice(y0 - HALO, y1 - HALO)
+                new = new[y0 - x0 : y1 - x0]
+                if s + 1 == ITERS:
+                    O[f, at, 8 * k : 8 * k + 8] = new
+                gap = D[f, at, 8 * k : 8 * k + 8] - new
+                acc = acc + jnp.sum(gap * gap, axis=0)
+        return acc
+
+    def diffuse_inner(f):
+        for s in range(ITERS):
+            ACC[s * fields + f] = update(f, s, [(HALO + 1 + s, HALO + cols - 1 - s)], INNER_STRIPS)
+
+    def diffuse_edges(f):
         both_ends(U.at[f, west, body_rows], EDGE, edge_sem.at[0, f]).wait_recv()
         both_ends(U.at[f, east_edge, body_rows], EDGE, edge_sem.at[1, f]).wait_recv()
         outside(U, f)
         for s in range(ITERS):
-            src = U.at[f] if s == 0 else W.at[(s - 1) % 2]
-            lo, hi = s + 1, wide - (s + 1)
-            cuts = [lo + (hi - lo) * i // STRIPS for i in range(STRIPS + 1)]
-            acc = jnp.zeros((8, LANES), F32)
-            for k in range(blocks):
-                r = PAD + 8 * k
-                for x0, x1 in zip(cuts[:-1], cuts[1:]):
-                    near = src[x0 - 1 : x1 + 1, r : r + 8]
-                    cur = near[1:-1]
-                    lane = iota((x1 - x0, 8, LANES), 2)
-                    below = src[x0:x1, r - 4 : r + 4]
-                    above = src[x0:x1, r + 4 : r + 12]
-                    south = pltpu.roll(jnp.where(lane == LANES - 1, below, cur), 1, 2)
-                    north_of = pltpu.roll(jnp.where(lane == 0, above, cur), LANES - 1, 2)
-                    around = (near[:-2] + near[2:]) + (south + north_of)
-                    new = (1.0 - 4.0 * DIFFUSION) * cur + DIFFUSION * around
-                    if s + 1 < ITERS:
-                        W[s % 2, x0:x1, r : r + 8] = new
-                    y0, y1 = max(x0, HALO), min(x1, HALO + cols)
-                    if y0 >= y1:
-                        continue
-                    at = slice(y0 - HALO, y1 - HALO)
-                    new = new[y0 - x0 : y1 - x0]
-                    if s + 1 == ITERS:
-                        O[f, at, 8 * k : 8 * k + 8] = new
-                    gap = D[f, at, 8 * k : 8 * k + 8] - new
-                    acc = acc + jnp.sum(gap * gap, axis=0)
+            spans = [(s + 1, HALO + 1 + s), (HALO + cols - 1 - s, wide - 1 - s)]
+            acc = update(f, s, spans, 1)
+            ACC[s * fields + f] = ACC[s * fields + f] + acc
             if s + 1 < ITERS:
-                outside(W, s % 2)
-            ACC[s * fields + f] = acc
-
-    diffuse(0)
-    both_ends(RA.at[pl.ds(0, members - 1)], SLICE).wait_recv()
-    total = RA[0]
-    for i in range(1, members):
-        total = total + RA[i]
-    turned = pltpu.roll(total, 64, 1)
-    left_half = lane16 < 64
-    r_part = jnp.where(left_half, total[0:16], turned[16:32])
-    d_part = jnp.where(left_half, turned[0:16], total[16:32])
-    for i in range(RING):
-        part = slice(i * share, (i + 1) * share)
-        XP[i] = jnp.concatenate([r_part[part], d_part[part]], axis=0)
-    for i in spots:
-        send(XP.at[i], XB.at[z], SHARE, ring(i))
-    QB[z] = substeps(*all_modes, r_part, d_part)[-1][0]
-    for i in spots:
-        send(QB.at[z], QB.at[z], SUM, ring(i))
-    XB[z] = XP[z]
-    lax.fori_loop(1, fields, lambda f, c: (diffuse(f), c)[1], 0)
-
-    both_ends(XB.at[pl.ds(0, RING - 1)], SHARE).wait_recv()
-    shares = XB[0]
-    for i in range(1, RING):
-        shares = shares + XB[i]
+                outside(W, f, s)
+
+    send(XD.at[CORES - 1 - core], PX, PAIR, partner)
+    rim = jnp.zeros((wide, PAD, LANES), F32)
+    for f in range(fields):
+        for ref in [U.at[f]] + [W.at[f, s] for s in range(ITERS - 1)]:
+            ref[:, 0:PAD] = rim
+            ref[:, PAD + rows : high_rows] = rim
+    lax.fori_loop(0, AHEAD, lambda f, c: (diffuse_inner(f), c)[1], 0)
+    both_ends(PX, PAIR).wait_recv()
+    total = XD[core] + PX[...]
+    for i in range(chips):
+        l, top = (i * share) // 16, (i * share) % 16
+        XS[i, :share] = total[32 * l + top : 32 * l + top + share]
+        XS[i, share:] = total[32 * l + 16 + top : 32 * l + 16 + top + share]
+    for i in range(2, len(rounds)):
+        hear(i)
+        tell(i + 1)
+    for i in others:
+        send(XS.at[i], XB.at[chip], SHARE, peer(i))
+    XB[chip] = XS[chip]
+    lax.fori_loop(AHEAD, fields, lambda f, c: (diffuse_inner(f), c)[1], 0)
+    lax.fori_loop(0, fields, lambda f, c: (diffuse_edges(f), c)[1], 0)
+
+    both_ends(XB.at[pl.ds(0, chips - 1)], SHARE).wait_recv()
+    shares = jnp.sum(XB[...], axis=0)
     r_sum, d_sum = shares[:share], shares[share:]
     energy = jnp.zeros((16, LANES), F32)
     weight = -0.25 * (east + 1.0) * (north + 1.0)
     my_field = jnp.where(lane16 % 64 >= 32, f_low + 1, f_low)
-    for s, (t, r, v) in enumerate(substeps(*my_modes, r_sum, d_sum)):
+    course = substeps(*my_modes, r_sum, d_sum)
+    for s, (t, r, v) in enumerate(course):
         part = jnp.sum(weight * t * (r + v), axis=0, keepdims=True)
         energy = jnp.where(row16 == s * fields + my_field, part, energy)
     for i in range(ITERS * fields):
         energy = energy + jnp.where(row16 == i, jnp.sum(ACC[i], axis=0, keepdims=True), 0.0)
     energy = jnp.sum(energy, axis=1, keepdims=True)
-    SB[z] = jnp.sum(jnp.where(row16 == lane16, energy, 0.0), axis=0, keepdims=True)
-    for i in spots:
-        send(SB.at[z], SB.at[z], PART, ring(i))
-
-    both_ends(QB.at[pl.ds(0, RING - 1)], SUM).wait_recv()
-    q_sum = QB[0]
-    for i in range(1, RING):
-        q_sum = q_sum + QB[i]
-    QC[me] = q_sum
+    Y[chip, :share] = course[-1][0]
+    Y[chip, share:] = jnp.sum(jnp.where(row16 == lane16, energy, 0.0), axis=0, keepdims=True)
     for i in others:
-        send(QC.at[me], QC.at[me], BACK, member(i))
-
-    both_ends(QC.at[pl.ds(0, members - 1)], BACK).wait_recv()
+        send(Y.at[chip], Y.at[chip], ALL, peer(i))
+    both_ends(Y.at[pl.ds(0, chips - 1)], ALL).wait_recv()
+    send(Y, YP, BACK, partner)
+    for i in range(chips):
+        QD[core, i * share : (i + 1) * share] = Y[i, :share]
+
+    both_ends(YP, BACK).wait_recv()
+    for i in range(chips):
+        QD[CORES - 1 - core, i * share : (i + 1) * share] = YP[i, :share]
     for h in range(fields // 2):
         parts = []
         for l in range(levels):
-            packed = QC[h * levels + l]
+            packed = QD[h, 16 * l : 16 * l + 16]
             parts += [packed, pltpu.roll(packed, 64, 1)]
         modal = jnp.dot(
             to_grid, jnp.concatenate(parts, axis=0), precision=HIGHEST, preferred_element_type=F32
@@ -375,17 +392,7 @@
                 at = pl.ds(8 * (k + i), 8)
                 O[f, :, at] = O[f, :, at] + tend[:, i * LANES : (i + 1) * LANES].reshape(cols, 8, LANES)
 
-    both_ends(SB.at[pl.ds(0, RING - 1)], PART).wait_recv()
-    sums = SB[0]
-    for i in range(1, RING):
-        sums = sums + SB[i]
-    EB[me] = sums
-    for i in others:
-        send(EB.at[me], EB.at[me], LOG, member(i))
-    both_ends(EB.at[pl.ds(0, members - 1)], LOG).wait_recv()
-    sums = EB[0]
-    for i in range(1, members):
-        sums = sums + EB[i]
+    sums = jnp.sum(Y[:, share:], axis=0) + jnp.sum(YP[:, share:], axis=0)
     cells = float(levels * east * north)
     value = jnp.broadcast_to(jnp.sqrt(jnp.maximum(sums / cells, 0.0)), (8, LANES))
     row8 = iota((8, LANES), 0)
@@ -395,8 +402,10 @@
     log_ref[...] = log
 
     both_ends(U.at[:, pl.ds(0, 2 * HALO), body_rows], EDGE).wait_send()
-    for phase, buf in ((SLICE, RA), (SHARE, XB), (SUM, QB), (BACK, QC), (PART, SB), (LOG, EB)):
-        both_ends(buf.at[pl.ds(0, buf.shape[0] - 1)], phase).wait_send()
+    both_ends(PX, PAIR).wait_send()
+    both_ends(XB.at[pl.ds(0, chips - 1)], SHARE).wait_send()
+    both_ends(Y.at[pl.ds(0, chips - 1)], ALL).wait_send()
+    both_ends(YP, BACK).wait_send()
 
 
 def writer(O, log_ref, o_hbm, res_ref, sem):
@@ -413,13 +422,13 @@
 
 def solution(mesh):
     tiles = mesh.shape["gx"]
-    members = tiles // RING
+    chips = tiles // CORES
 
     def local(model_state, driving, mode_east, mode_north, level_class, nudge_table):
         fields, levels, cols, north = model_state.shape
         rows = levels * north // LANES
         wide, high_rows = cols + 2 * HALO, rows + 2 * PAD
-        share = 16 // RING
+        share = 16 * levels // chips
         vm = lambda *shape: pltpu.VMEM(shape, F32)
         dma = lambda *shape: pltpu.SemaphoreType.DMA(shape)
         hbm = pl.BlockSpec(memory_space=pltpu.HBM)
@@ -428,12 +437,12 @@
         scratch = [
             smem(mode_east), smem(mode_north), smem(level_class), smem(table),
             vm(fields, wide, high_rows, LANES), vm(fields, cols, rows, LANES),
-            vm(2, wide, high_rows, LANES), pltpu.VMEM((LANES, north), jnp.bfloat16),
-            vm(members, 32, LANES), vm(members, 32, LANES),
-            vm(RING, 16, LANES), vm(RING, 2 * share, LANES), vm(RING, 2 * share, LANES), vm(members, 16, LANES),
-            vm(RING, 1, LANES), vm(members, 1, LANES),
+            vm(fields, ITERS - 1, wide, high_rows, LANES), pltpu.VMEM((LANES, north), jnp.bfloat16),
+            vm(CORES, 32 * levels, LANES), vm(32 * levels, LANES),
+            vm(chips, 2 * share, LANES), vm(chips, 2 * share, LANES),
+            vm(chips, share + 1, LANES), vm(chips, share + 1, LANES), vm(CORES, 16 * levels, LANES),
             vm(ITERS * fields, 8, LANES), pltpu.VMEM((fields, 8 * cols, 2 * LANES), jnp.bfloat16),
-            dma(4), dma(2, fields // 2), dma(2, fields), dma(2, 7),
+            dma(4), dma(2, fields // 2), dma(2, fields), dma(2, 5), pltpu.SemaphoreType.REGULAR((4,)),
         ]
         turn = (0, 2, 1, 3)
         inner = pl.BlockSpec(memory_space=pltpu.VMEM)

time: 60.4 us -> 58.9 us (0.975)
  Pallas kernels: 59.7 us -> 58.2 us
    pallas_call x1, Pallas kernels: 57.4 us -> 55.9 us  [local(): pl.pallas_call(functools.partial(kernel, tiles), out_shape=(vm(fields, co...]
where the time goes in v3:
time: 58.9 us; the launch traced here: 58.8 us
  Pallas kernels  58.2 us (99%)
  between operations  0.64 us (1%)
    pallas_call x1, Pallas kernels, local(): pl.pallas_call(functools.partial(kernel, tiles), out_shape=(vm(fields, co...  55.9 us
    pallas_call x1, Pallas kernels, local(): pl.pallas_call(writer, out_shape=(jax.ShapeDtypeStruct((fields, cols, lev...  2.27 us

profile of v3, /device:TPU:33, one launch (start us, length us, event | category | flops | bytes accessed | tf_op | source)
XLA Modules:
  0.0 58.8 jit_solution(4352744493989549667)
XLA Ops:
  0.6 55.9 %shard_map.77 = (f32[4,20,80,128]{3,2,1,0:T(8,128)S(1)}, f32[8,128]{1,0:T(8,128)S(1)}) custom-call(f32[4,20,4,2560]{3,2,1,0:T(4,128)} %bitcast.4, f32[4,20,4,2560]{3,2,1,0:T(4,128)} %bitcast.5, s32[30]{0:T(128)} %me_hbm.1, s32[30]{0:T(128)} %mn_hbm.1, s32[4]{0:T(128)} %lc_hbm.1, f32[4,8]{1,0:T(4,128)} %bitcast.6), custom_call_target="tpu_custom_call" | custom-call | tf_op jit(solution)/shard_map/pallas_call | solution.py:449
  56.6 2.3 %shard_map.78 = (f32[4,20,4,2560]{3,2,1,0:T(4,128)}, f32[4,4]{1,0:T(4,128)}) custom-call(f32[4,20,80,128]{3,2,1,0:T(8,128)S(1)} %get-tuple-element.6.O, f32[8,128]{1,0:T(8,128)S(1)} %get-tuple-element.7.log_ref), custom_call_target="tpu_custom_call" | custom-call | tf_op jit(solution)/shard_map/pallas_call | solution.py:465

commit v4 on v3

--- a/solution.py
+++ b/solution.py
@@ -212,6 +212,10 @@
     contract_lanes = (((1,), (1,)), ((), ()))
     for h in range(0, fields, 2):
         loaded(0, h)
+        for f in range(h, min(h + 2, fields - 1)):
+            send_edges(f)
+        hear(h // 2)
+        tell(h // 2 + 1)
         loaded(1, h)
         acc_r = acc_d = None
         held = []
@@ -251,10 +255,6 @@
             mix = jnp.concatenate([mix, jnp.zeros((grid_rows - count, LANES), F32)], axis=0)
         modal = norm * jnp.dot(to_modes, mix, precision=HIGHEST, preferred_element_type=F32)
         turned = pltpu.roll(modal, 64, 1)
-        send_edges(h)
-        send_edges(h + 1)
-        hear(h // 2)
-        tell(h // 2 + 1)
         for l in range(levels):
             upper_a, lower_a = slice(32 * l, 32 * l + 16), slice(32 * l + 16, 32 * l + 32)
             XD[h // 2, 32 * l : 32 * l + 16] = jnp.where(lane16 < 64, modal[upper_a], turned[lower_a])
@@ -335,6 +335,7 @@
         tell(i + 1)
     for i in others:
         send(XS.at[i], XB.at[chip], SHARE, peer(i))
+    send_edges(fields - 1)
     XB[chip] = XS[chip]
     lax.fori_loop(AHEAD, fields, lambda f, c: (diffuse_inner(f), c)[1], 0)
     lax.fori_loop(0, fields, lambda f, c: (diffuse_edges(f), c)[1], 0)

time: 58.9 us -> 55.6 us (0.944)
  Pallas kernels: 58.2 us -> 54.8 us
    pallas_call x1, Pallas kernels: 55.9 us -> 52.5 us  [local(): pl.pallas_call(functools.partial(kernel, tiles), out_shape=(vm(fields, co...]
where the time goes in v4:
time: 55.6 us; the launch traced here: 55.5 us
  Pallas kernels  54.8 us (99%)
  between operations  0.64 us (1%)
    pallas_call x1, Pallas kernels, local(): pl.pallas_call(functools.partial(kernel, tiles), out_shape=(vm(fields, co...  52.5 us
    pallas_call x1, Pallas kernels, local(): pl.pallas_call(writer, out_shape=(jax.ShapeDtypeStruct((fields, cols, lev...  2.27 us

profile of v4, /device:TPU:33, one launch (start us, length us, event | category | flops | bytes accessed | tf_op | source)
XLA Modules:
  0.0 55.5 jit_solution(1527369113598049065)
XLA Ops:
  0.6 52.5 %shard_map.77 = (f32[4,20,80,128]{3,2,1,0:T(8,128)S(1)}, f32[8,128]{1,0:T(8,128)S(1)}) custom-call(f32[4,20,4,2560]{3,2,1,0:T(4,128)} %bitcast.4, f32[4,20,4,2560]{3,2,1,0:T(4,128)} %bitcast.5, s32[30]{0:T(128)} %me_hbm.1, s32[30]{0:T(128)} %mn_hbm.1, s32[4]{0:T(128)} %lc_hbm.1, f32[4,8]{1,0:T(4,128)} %bitcast.6), custom_call_target="tpu_custom_call" | custom-call | tf_op jit(solution)/shard_map/pallas_call | solution.py:450
  53.2 2.3 %shard_map.78 = (f32[4,20,4,2560]{3,2,1,0:T(4,128)}, f32[4,4]{1,0:T(4,128)}) custom-call(f32[4,20,80,128]{3,2,1,0:T(8,128)S(1)} %get-tuple-element.6.O, f32[8,128]{1,0:T(8,128)S(1)} %get-tuple-element.7.log_ref), custom_call_target="tpu_custom_call" | custom-call | tf_op jit(solution)/shard_map/pallas_call | solution.py:466

commit v5 on v4

--- a/solution.py
+++ b/solution.py
@@ -207,6 +207,63 @@
         send(U.at[f, inner_east, body_rows], U.at[f, west, body_rows], EDGE, right, edge_sem.at[0, f])
         send(U.at[f, inner_west, body_rows], U.at[f, east_edge, body_rows], EDGE, left, edge_sem.at[1, f])
 
+    def outside(ref, *at):
+        hollow = jnp.zeros((HALO, rows, LANES), F32)
+
+        @pl.when(g == 0)
+        def _():
+            ref[(*at, pl.ds(0, HALO), body_rows)] = hollow
+
+        @pl.when(g == tiles - 1)
+        def _():
+            ref[(*at, pl.ds(HALO + cols, HALO), body_rows)] = hollow
+
+    def update(f, s, bounds, strips):
+        src = U.at[f] if s == 0 else W.at[f, s - 1]
+        acc = jnp.zeros((8, LANES), F32)
+        cuts = []
+        for lo, hi in bounds:
+            cuts += [(lo + (hi - lo) * i // strips, lo + (hi - lo) * (i + 1) // strips) for i in range(strips)]
+        for k in range(blocks):
+            r = PAD + 8 * k
+            for x0, x1 in cuts:
+                near = src[x0 - 1 : x1 + 1, r : r + 8]
+                cur = near[1:-1]
+                lane = iota((x1 - x0, 8, LANES), 2)
+                below = src[x0:x1, r - 4 : r + 4]
+                above = src[x0:x1, r + 4 : r + 12]
+                south = pltpu.roll(jnp.where(lane == LANES - 1, below, cur), 1, 2)
+                north_of = pltpu.roll(jnp.where(lane == 0, above, cur), LANES - 1, 2)
+                around = (near[:-2] + near[2:]) + (south + north_of)
+                new = (1.0 - 4.0 * DIFFUSION) * cur + DIFFUSION * around
+                if s + 1 < ITERS:
+                    W[f, s, x0:x1, r : r + 8] = new
+                y0, y1 = max(x0, HALO), min(x1, HALO + cols)
+                if y0 >= y1:
+                    continue
+                at = slice(y0 - HALO, y1 - HALO)
+                new = new[y0 - x0 : y1 - x0]
+                if s + 1 == ITERS:
+                    O[f, at, 8 * k : 8 * k + 8] = new
+                gap = D[f, at, 8 * k : 8 * k + 8] - new
+                acc = acc + jnp.sum(gap * gap, axis=0)
+        return acc
+
+    def diffuse_inner(f):
+        for s in range(ITERS):
+            ACC[s * fields + f] = update(f, s, [(HALO + 1 + s, HALO + cols - 1 - s)], INNER_STRIPS)
+
+    def diffuse_edges(f):
+        both_ends(U.at[f, west, body_rows], EDGE, edge_sem.at[0, f]).wait_recv()
+        both_ends(U.at[f, east_edge, body_rows], EDGE, edge_sem.at[1, f]).wait_recv()
+        outside(U, f)
+        for s in range(ITERS):
+            spans = [(s + 1, HALO + 1 + s), (HALO + cols - 1 - s, wide - 1 - s)]
+            acc = update(f, s, spans, 1)
+            ACC[s * fields + f] = ACC[s * fields + f] + acc
+            if s + 1 < ITERS:
+                outside(W, f, s)
+
     norm = 4.0 / ((east + 1) * (north + 1))
     odd_chunk = row_g % 8 >= 4
     contract_lanes = (((1,), (1,)), ((), ()))
@@ -214,9 +271,16 @@
         loaded(0, h)
         for f in range(h, min(h + 2, fields - 1)):
             send_edges(f)
+        loaded(1, h)
+        if h == 0:
+            rim = jnp.zeros((wide, PAD, LANES), F32)
+            for f in range(fields):
+                for ref in [U.at[f]] + [W.at[f, s] for s in range(ITERS - 1)]:
+                    ref[:, 0:PAD] = rim
+                    ref[:, PAD + rows : high_rows] = rim
+            lax.fori_loop(0, AHEAD, lambda f, c: (diffuse_inner(f), c)[1], 0)
         hear(h // 2)
         tell(h // 2 + 1)
-        loaded(1, h)
         acc_r = acc_d = None
         held = []
         for k in range(blocks):
@@ -260,70 +324,7 @@
             XD[h // 2, 32 * l : 32 * l + 16] = jnp.where(lane16 < 64, modal[upper_a], turned[lower_a])
             XD[h // 2, 32 * l + 16 : 32 * l + 32] = jnp.where(lane16 < 64, turned[upper_a], modal[lower_a])
 
-    def outside(ref, *at):
-        hollow = jnp.zeros((HALO, rows, LANES), F32)
-
-        @pl.when(g == 0)
-        def _():
-            ref[(*at, pl.ds(0, HALO), body_rows)] = hollow
-
-        @pl.when(g == tiles - 1)
-        def _():
-            ref[(*at, pl.ds(HALO + cols, HALO), body_rows)] = hollow
-
-    def update(f, s, bounds, strips):
-        src = U.at[f] if s == 0 else W.at[f, s - 1]
-        acc = jnp.zeros((8, LANES), F32)
-        cuts = []
-        for lo, hi in bounds:
-            cuts += [(lo + (hi - lo) * i // strips, lo + (hi - lo) * (i + 1) // strips) for i in range(strips)]
-        for k in range(blocks):
-            r = PAD + 8 * k
-            for x0, x1 in cuts:
-                near = src[x0 - 1 : x1 + 1, r : r + 8]
-                cur = near[1:-1]
-                lane = iota((x1 - x0, 8, LANES), 2)
-                below = src[x0:x1, r - 4 : r + 4]
-                above = src[x0:x1, r + 4 : r + 12]
-                south = pltpu.roll(jnp.where(lane == LANES - 1, below, cur), 1, 2)
-                north_of = pltpu.roll(jnp.where(lane == 0, above, cur), LANES - 1, 2)
-                around = (near[:-2] + near[2:]) + (south + north_of)
-                new = (1.0 - 4.0 * DIFFUSION) * cur + DIFFUSION * around
-                if s + 1 < ITERS:
-                    W[f, s, x0:x1, r : r + 8] = new
-                y0, y1 = max(x0, HALO), min(x1, HALO + cols)
-                if y0 >= y1:
-                    continue
-                at = slice(y0 - HALO, y1 - HALO)
-                new = new[y0 - x0 : y1 - x0]
-                if s + 1 == ITERS:
-                    O[f, at, 8 * k : 8 * k + 8] = new
-                gap = D[f, at, 8 * k : 8 * k + 8] - new
-                acc = acc + jnp.sum(gap * gap, axis=0)
-        return acc
-
-    def diffuse_inner(f):
-        for s in range(ITERS):
-            ACC[s * fields + f] = update(f, s, [(HALO + 1 + s, HALO + cols - 1 - s)], INNER_STRIPS)
-
-    def diffuse_edges(f):
-        both_ends(U.at[f, west, body_rows], EDGE, edge_sem.at[0, f]).wait_recv()
-        both_ends(U.at[f, east_edge, body_rows], EDGE, edge_sem.at[1, f]).wait_recv()
-        outside(U, f)
-        for s in range(ITERS):
-            spans = [(s + 1, HALO + 1 + s), (HALO + cols - 1 - s, wide - 1 - s)]
-            acc = update(f, s, spans, 1)
-            ACC[s * fields + f] = ACC[s * fields + f] + acc
-            if s + 1 < ITERS:
-                outside(W, f, s)
-
     send(XD.at[CORES - 1 - core], PX, PAIR, partner)
-    rim = jnp.zeros((wide, PAD, LANES), F32)
-    for f in range(fields):
-        for ref in [U.at[f]] + [W.at[f, s] for s in range(ITERS - 1)]:
-            ref[:, 0:PAD] = rim
-            ref[:, PAD + rows : high_rows] = rim
-    lax.fori_loop(0, AHEAD, lambda f, c: (diffuse_inner(f), c)[1], 0)
     both_ends(PX, PAIR).wait_recv()
     total = XD[core] + PX[...]
     for i in range(chips):

time: 55.6 us -> 56 us (level)
  no operation moved by 1% of the time
where the time goes in v5:
time: 56 us; the launch traced here: 55.9 us
  Pallas kernels  55.3 us (99%)
  between operations  0.64 us (1%)
    pallas_call x1, Pallas kernels, local(): pl.pallas_call(functools.partial(kernel, tiles), out_shape=(vm(fields, co...  53 us
    pallas_call x1, Pallas kernels, local(): pl.pallas_call(writer, out_shape=(jax.ShapeDtypeStruct((fields, cols, lev...  2.27 us

profile of v5, /device:TPU:33, one launch (start us, length us, event | category | flops | bytes accessed | tf_op | source)
XLA Modules:
  0.0 55.9 jit_solution(16302383781506161925)
XLA Ops:
  0.6 53.0 %shard_map.77 = (f32[4,20,80,128]{3,2,1,0:T(8,128)S(1)}, f32[8,128]{1,0:T(8,128)S(1)}) custom-call(f32[4,20,4,2560]{3,2,1,0:T(4,128)} %bitcast.4, f32[4,20,4,2560]{3,2,1,0:T(4,128)} %bitcast.5, s32[30]{0:T(128)} %me_hbm.1, s32[30]{0:T(128)} %mn_hbm.1, s32[4]{0:T(128)} %lc_hbm.1, f32[4,8]{1,0:T(4,128)} %bitcast.6), custom_call_target="tpu_custom_call" | custom-call | tf_op jit(solution)/shard_map/pallas_call | solution.py:451
  53.6 2.3 %shard_map.78 = (f32[4,20,4,2560]{3,2,1,0:T(4,128)}, f32[4,4]{1,0:T(4,128)}) custom-call(f32[4,20,80,128]{3,2,1,0:T(8,128)S(1)} %get-tuple-element.6.O, f32[8,128]{1,0:T(8,128)S(1)} %get-tuple-element.7.log_ref), custom_call_target="tpu_custom_call" | custom-call | tf_op jit(solution)/shard_map/pallas_call | solution.py:467
